TPU v7x, 32 devices: a whole 2x2x4 slice. The times are simulated.
32 devices in a mesh: dp: 8 (over y, x, core), tensor: 4 (over z).
Axes of the slice: x: 2, y: 2, z: 4, core: 2. Of those that a mesh axis runs over, the one named last changes fastest.
Arguments:
- tokens_in: bfloat16 [8192, 1024], P(('dp', 'tensor')), may hold values from -6 to 6
- starts: int32 [8, 4], P('dp'), may hold values from 0 to 768, as said below
- ln1_gain: float32 [1024], P(('dp', 'tensor')), may hold values from 0.25 to 1.75
- ln1_bias: float32 [1024], P(('dp', 'tensor')), may hold values from -4 to 4
- w_qkv: bfloat16 [1024, 3072], P('dp', 'tensor'), may hold values from -0.25 to 0.25
- b_qv: bfloat16 [128, 16], P('tensor', 'dp'), may hold values from -6 to 6
- w_out: bfloat16 [1024, 1024], P('tensor', 'dp'), may hold values from -0.75 to 0.75
- b_out: float32 [1024], P(('dp', 'tensor')), may hold values from -6 to 6
- ln2_gain: float32 [1024], P(('dp', 'tensor')), may hold values from 0.25 to 1.75
- ln2_bias: float32 [1024], P(('dp', 'tensor')), may hold values from -4 to 4
- w_up: bfloat16 [1024, 4096], P('dp', 'tensor'), may hold values from -0.1875 to 0.1875
- b_up: bfloat16 [256, 16], P('tensor', 'dp'), may hold values from -6 to 6
- w_down: bfloat16 [4096, 1024], P('tensor', 'dp'), may hold values from -0.09375 to 0.09375
- b_down: float32 [1024], P(('dp', 'tensor')), may hold values from -6 to 6
- grad_out: bfloat16 [8192, 1024], P(('dp', 'tensor')), may hold values from -6 to 6
Outputs:
- output: bfloat16 [8192, 1024], P(('dp', 'tensor'))
- grad_tokens: bfloat16 [8192, 1024], P(('dp', 'tensor'))
- grad_ln1_gain: float32 [1024], P(('dp', 'tensor'))
- grad_ln1_bias: float32 [1024], P(('dp', 'tensor'))
- grad_w_qkv: float32 [1024, 3072], P('dp', 'tensor')
- grad_b_qv: float32 [128, 16], P('tensor', 'dp')
- grad_w_out: float32 [1024, 1024], P('tensor', 'dp')
- grad_b_out: float32 [1024], P(('dp', 'tensor'))
- grad_ln2_gain: float32 [1024], P(('dp', 'tensor'))
- grad_ln2_bias: float32 [1024], P(('dp', 'tensor'))
- grad_w_up: float32 [1024, 4096], P('dp', 'tensor')
- grad_b_up: float32 [256, 16], P('tensor', 'dp')
- grad_w_down: float32 [4096, 1024], P('tensor', 'dp')
- grad_b_down: float32 [1024], P(('dp', 'tensor'))
Inputs may be any that keep to these rules, and one draw needn't show every extreme that they name: starts[s, p] lies in the p-th of 4 equal regions of the sequence, and the span of 256 tokens from it ends inside that region.
All inputs are finite; a program needn't handle non-finite values.
Results may differ from a plain program's by a relative error of at most 0.02.
Values may be sent and summed in bfloat16 or wider, within the bound.
A program may use at most 128 MiB of HBM per device.

v0:
```python
import jax
import jax.numpy as jnp
from jax import lax
from jax.sharding import PartitionSpec as P

HD = 64
PIECE = 256
QBLOCK = 512


EPS = 1e-05
ROOT = 0.7978845608028654


def gelu_tanh(values):
    return 0.5 * values * (1.0 + jnp.tanh(ROOT * (values + 0.044715 * values * values * values)))


def normalize(values):
    center = jnp.mean(values, axis=-1, keepdims=True)
    shifted = values - center
    inverse = lax.rsqrt(jnp.mean(shifted * shifted, axis=-1, keepdims=True) + EPS)
    return (shifted * inverse, inverse)


def norm_back(grad_normed, normed, inverse, gain):
    scaled = grad_normed * gain
    return inverse * (
        scaled
        - jnp.mean(scaled, axis=-1, keepdims=True)
        - normed * jnp.mean(scaled * normed, axis=-1, keepdims=True)
    )


def dot_last(left, right):
    return lax.dot_general(
        left, right, (((1,), (1,)), ((), ())), preferred_element_type=jnp.float32
    )


def dot_first(left, right):
    return lax.dot_general(
        left, right, (((0,), (0,)), ((), ())), preferred_element_type=jnp.float32
    )


def gather_rows(values):
    return lax.all_gather(values, "tensor", axis=0, tiled=True)


def gather_grads(values):
    return lax.all_gather(values, "tensor", axis=0, tiled=True)


def reduce_rows(left, weight, rows):

    def term(start, count):
        return jnp.dot(left, weight, preferred_element_type=jnp.float32)

    return lax.psum_scatter(
        term(jnp.int32(0), lax.axis_size("tensor") * rows).astype(jnp.bfloat16),
        "tensor",
        scatter_dimension=0,
        tiled=True,
    ).astype(jnp.float32)


def reduce_grads(left, weight, rows):

    def term(start, count):
        return dot_last(left, weight)

    return lax.psum_scatter(
        term(jnp.int32(0), lax.axis_size("tensor") * rows).astype(jnp.bfloat16),
        "tensor",
        scatter_dimension=0,
        tiled=True,
    ).astype(jnp.float32)


def piece_ids(start_row, length):
    places = jnp.arange(length, dtype=jnp.int32)
    inside = (places[:, None] >= start_row[None, :]) & (
        places[:, None] < start_row[None, :] + PIECE
    )
    labels = jnp.arange(1, start_row.shape[0] + 1, dtype=jnp.int32)
    return jnp.sum(jnp.where(inside, labels[None, :], 0), axis=1)


def allowed_block(row_ids, row_places, key_ids, key_places):
    causal = key_places[None, :] <= row_places[:, None]
    picture = (row_ids[:, None] == key_ids[None, :]) & (row_ids[:, None] > 0)
    return causal | picture


def block_scores(by_seq, start_rows, block_index):
    length = by_seq.shape[1]
    per_seq = length // QBLOCK
    seq_index = block_index // per_seq
    first_row = block_index % per_seq * QBLOCK
    sequence = lax.dynamic_index_in_dim(by_seq, seq_index, 0, keepdims=False)
    key_ids = piece_ids(lax.dynamic_index_in_dim(start_rows, seq_index, 0, keepdims=False), length)
    query_rows = lax.dynamic_slice_in_dim(sequence, first_row, QBLOCK, 0)[:, :, 0]
    key_rows = sequence[:, :, 1]
    value_rows = sequence[:, :, 2]
    row_ids = lax.dynamic_slice_in_dim(key_ids, first_row, QBLOCK, 0)
    row_places = first_row + jnp.arange(QBLOCK, dtype=jnp.int32)
    scores = (
        jnp.einsum("qhd,khd->hqk", query_rows, key_rows, preferred_element_type=jnp.float32) * 0.125
    )
    places = jnp.arange(length, dtype=jnp.int32)
    scores = jnp.where(allowed_block(row_ids, row_places, key_ids, places)[None], scores, -1e30)
    return (seq_index, first_row, query_rows, key_rows, value_rows, scores)


def attention_forward(by_seq, start_rows):
    total_blocks = by_seq.shape[0] * (by_seq.shape[1] // QBLOCK)

    def attend(block_index):
        _, _, query_rows, key_rows, value_rows, scores = block_scores(
            by_seq, start_rows, block_index
        )
        peak = jnp.max(scores, axis=-1, keepdims=True)
        log_total = peak + jnp.log(jnp.sum(jnp.exp(scores - peak), axis=-1, keepdims=True))
        probs = jnp.exp(scores - log_total)
        heads = jnp.einsum(
            "hqk,khd->qhd",
            probs.astype(jnp.bfloat16),
            value_rows,
            preferred_element_type=jnp.float32,
        )
        return (heads.astype(jnp.bfloat16), log_total)

    return lax.map(attend, jnp.arange(total_blocks, dtype=jnp.int32))


def attention_backward(by_seq, start_rows, log_totals, grad_heads):
    total_blocks = by_seq.shape[0] * (by_seq.shape[1] // QBLOCK)
    empty = jnp.zeros(by_seq.shape[:3] + (HD,), jnp.float32)

    def step(carry, item):
        grad_keys, grad_values = carry
        block_index, log_total = item
        seq_index, first_row, query_rows, key_rows, value_rows, scores = block_scores(
            by_seq, start_rows, block_index
        )
        grad_seq = lax.dynamic_index_in_dim(grad_heads, seq_index, 0, keepdims=False)
        grad_rows = lax.dynamic_slice_in_dim(grad_seq, first_row, QBLOCK, 0)
        probs = jnp.exp(scores - log_total)
        grad_probs = jnp.einsum(
            "qhd,khd->hqk", grad_rows, value_rows, preferred_element_type=jnp.float32
        )
        inner = jnp.sum(probs * grad_probs, axis=-1, keepdims=True)
        grad_scores = (probs * (grad_probs - inner)).astype(jnp.bfloat16)
        grad_query = (
            jnp.einsum("hqk,khd->qhd", grad_scores, key_rows, preferred_element_type=jnp.float32)
            * 0.125
        )
        key_term = (
            jnp.einsum("hqk,qhd->khd", grad_scores, query_rows, preferred_element_type=jnp.float32)
            * 0.125
        )
        value_term = jnp.einsum(
            "hqk,qhd->khd",
            probs.astype(jnp.bfloat16),
            grad_rows,
            preferred_element_type=jnp.float32,
        )
        grad_keys = lax.dynamic_update_index_in_dim(
            grad_keys,
            lax.dynamic_index_in_dim(grad_keys, seq_index, 0, keepdims=False) + key_term,
            seq_index,
            0,
        )
        grad_values = lax.dynamic_update_index_in_dim(
            grad_values,
            lax.dynamic_index_in_dim(grad_values, seq_index, 0, keepdims=False) + value_term,
            seq_index,
            0,
        )
        return ((grad_keys, grad_values), grad_query)

    (grad_keys, grad_values), grad_query = lax.scan(
        step, (empty, empty), (jnp.arange(total_blocks, dtype=jnp.int32), log_totals)
    )
    return (grad_query, grad_keys, grad_values)


def per_device(
    tokens_in,
    starts,
    ln1_gain,
    ln1_bias,
    w_qkv,
    b_qv,
    w_out,
    b_out,
    ln2_gain,
    ln2_bias,
    w_up,
    b_up,
    w_down,
    b_down,
    grad_out,
):
    rows = tokens_in.shape[0]
    gain_one, shift_one, bias_out, gain_two, shift_two, bias_down = (
        lax.all_gather(ln1_gain, ("dp", "tensor"), axis=0, tiled=True),
        lax.all_gather(ln1_bias, ("dp", "tensor"), axis=0, tiled=True),
        lax.all_gather(b_out, ("dp", "tensor"), axis=0, tiled=True),
        lax.all_gather(ln2_gain, ("dp", "tensor"), axis=0, tiled=True),
        lax.all_gather(ln2_bias, ("dp", "tensor"), axis=0, tiled=True),
        lax.all_gather(b_down, ("dp", "tensor"), axis=0, tiled=True),
    )
    weight_qkv, bias_qv, weight_out = (
        lax.all_gather(w_qkv, "dp", axis=0, tiled=True),
        lax.all_gather(b_qv, "dp", axis=1, tiled=True),
        lax.all_gather(w_out, "dp", axis=1, tiled=True),
    )
    weight_up, bias_up, weight_down = (
        lax.all_gather(w_up, "dp", axis=0, tiled=True),
        lax.all_gather(b_up, "dp", axis=1, tiled=True),
        lax.all_gather(w_down, "dp", axis=1, tiled=True),
    )
    local_heads = weight_qkv.shape[1] // (3 * HD)
    seq_count = starts.shape[0]
    inputs = tokens_in.astype(jnp.float32)
    normed_one, inverse_one = normalize(inputs)
    gathered_one = gather_rows((normed_one * gain_one + shift_one).astype(jnp.bfloat16))
    group = gathered_one.shape[0]
    length = group // seq_count
    bias_pair = bias_qv.astype(jnp.float32).reshape(local_heads, 2, HD)
    full_bias = jnp.stack(
        [bias_pair[:, 0], jnp.zeros_like(bias_pair[:, 0]), bias_pair[:, 1]], axis=1
    )
    projected = (
        jnp.dot(gathered_one, weight_qkv, preferred_element_type=jnp.float32).reshape(
            group, local_heads, 3, HD
        )
        + full_bias
    ).astype(jnp.bfloat16)
    by_seq = projected.reshape(seq_count, length, local_heads, 3, HD)
    heads_blocks, log_totals = attention_forward(by_seq, starts)
    heads_out = heads_blocks.reshape(group, local_heads * HD)
    middle = inputs + (reduce_rows(heads_out, weight_out, rows) + bias_out)
    normed_two, inverse_two = normalize(middle)
    rounded_two = (normed_two * gain_two + shift_two).astype(jnp.bfloat16)
    grad_final = grad_out.astype(jnp.float32)
    grad_bias_down = jnp.sum(grad_final, axis=0)
    gathered_two = gather_rows(rounded_two)
    up_proj = jnp.dot(gathered_two, weight_up, preferred_element_type=jnp.float32) + bias_up.astype(
        jnp.float32
    ).reshape(-1)
    hidden_act, gelu_pull = jax.vjp(gelu_tanh, up_proj)
    hidden_low = hidden_act.astype(jnp.bfloat16)
    output = (middle + reduce_rows(hidden_low, weight_down, rows) + bias_down).astype(jnp.bfloat16)
    grad_branch = gather_grads(grad_out)
    grad_w_down = dot_first(hidden_low, grad_branch)
    grad_up = gelu_pull(dot_last(grad_branch, weight_down))[0].astype(jnp.bfloat16)
    grad_b_up = jnp.sum(grad_up, axis=0, dtype=jnp.float32).reshape(bias_up.shape)
    grad_w_up = dot_first(gathered_two, grad_up)
    grad_two = reduce_grads(grad_up, weight_up, rows)
    grad_w_up, grad_b_up, grad_w_down = (
        lax.psum_scatter(
            grad_w_up.astype(jnp.bfloat16), "dp", scatter_dimension=0, tiled=True
        ).astype(jnp.float32),
        lax.psum_scatter(
            grad_b_up.astype(jnp.bfloat16), "dp", scatter_dimension=1, tiled=True
        ).astype(jnp.float32),
        lax.psum_scatter(
            grad_w_down.astype(jnp.bfloat16), "dp", scatter_dimension=1, tiled=True
        ).astype(jnp.float32),
    )
    grad_gain_two = jnp.sum(grad_two * normed_two, axis=0)
    grad_shift_two = jnp.sum(grad_two, axis=0)
    grad_middle = grad_final + norm_back(grad_two, normed_two, inverse_two, gain_two)
    grad_bias_out = jnp.sum(grad_middle, axis=0)
    grad_attn = gather_grads(grad_middle.astype(jnp.bfloat16))
    grad_w_out = dot_first(heads_out, grad_attn)
    grad_heads = (
        dot_last(grad_attn, weight_out)
        .astype(jnp.bfloat16)
        .reshape(seq_count, length, local_heads, HD)
    )
    grad_query, grad_keys, grad_values = attention_backward(by_seq, starts, log_totals, grad_heads)
    grad_proj = jnp.stack(
        [
            grad_query.reshape(group, local_heads, HD),
            grad_keys.reshape(group, local_heads, HD),
            grad_values.reshape(group, local_heads, HD),
        ],
        axis=2,
    ).astype(jnp.bfloat16)
    grad_b_qv = jnp.sum(grad_proj[:, :, 0::2], axis=0, dtype=jnp.float32).reshape(bias_qv.shape)
    grad_flat = grad_proj.reshape(group, 3 * local_heads * HD)
    grad_w_qkv = dot_first(gathered_one, grad_flat)
    grad_one = reduce_grads(grad_flat, weight_qkv, rows)
    grad_w_qkv, grad_b_qv, grad_w_out = (
        lax.psum_scatter(
            grad_w_qkv.astype(jnp.bfloat16), "dp", scatter_dimension=0, tiled=True
        ).astype(jnp.float32),
        lax.psum_scatter(
            grad_b_qv.astype(jnp.bfloat16), "dp", scatter_dimension=1, tiled=True
        ).astype(jnp.float32),
        lax.psum_scatter(
            grad_w_out.astype(jnp.bfloat16), "dp", scatter_dimension=1, tiled=True
        ).astype(jnp.float32),
    )
    grad_gain_one = jnp.sum(grad_one * normed_one, axis=0)
    grad_shift_one = jnp.sum(grad_one, axis=0)
    grad_tokens = (grad_middle + norm_back(grad_one, normed_one, inverse_one, gain_one)).astype(
        jnp.bfloat16
    )
    summed = (
        lax.psum_scatter(grad_gain_one, ("dp", "tensor"), scatter_dimension=0, tiled=True),
        lax.psum_scatter(grad_shift_one, ("dp", "tensor"), scatter_dimension=0, tiled=True),
        lax.psum_scatter(grad_bias_out, ("dp", "tensor"), scatter_dimension=0, tiled=True),
        lax.psum_scatter(grad_gain_two, ("dp", "tensor"), scatter_dimension=0, tiled=True),
        lax.psum_scatter(grad_shift_two, ("dp", "tensor"), scatter_dimension=0, tiled=True),
        lax.psum_scatter(grad_bias_down, ("dp", "tensor"), scatter_dimension=0, tiled=True),
    )
    return (
        output,
        grad_tokens,
        summed[0],
        summed[1],
        grad_w_qkv,
        grad_b_qv,
        grad_w_out,
        summed[2],
        summed[3],
        summed[4],
        grad_w_up,
        grad_b_up,
        grad_w_down,
        summed[5],
    )


def solution(mesh):
    return jax.shard_map(
        per_device,
        mesh=mesh,
        in_specs=(
            P(("dp", "tensor"), None),
            P("dp", None),
            P(("dp", "tensor")),
            P(("dp", "tensor")),
            P("dp", "tensor"),
            P("tensor", "dp"),
            P("tensor", "dp"),
            P(("dp", "tensor")),
            P(("dp", "tensor")),
            P(("dp", "tensor")),
            P("dp", "tensor"),
            P("tensor", "dp"),
            P("tensor", "dp"),
            P(("dp", "tensor")),
            P(("dp", "tensor"), None),
        ),
        out_specs=(
            P(("dp", "tensor"), None),
            P(("dp", "tensor"), None),
            P(("dp", "tensor")),
            P(("dp", "tensor")),
            P("dp", "tensor"),
            P("tensor", "dp"),
            P("tensor", "dp"),
            P(("dp", "tensor")),
            P(("dp", "tensor")),
            P(("dp", "tensor")),
            P("dp", "tensor"),
            P("tensor", "dp"),
            P("tensor", "dp"),
            P(("dp", "tensor")),
        ),
        check_vma=False,
    )
```

profile of v0, /device:TPU:1, one launch (start us, length us, event | category | flops | bytes accessed | tf_op | source)
XLA Modules:
  0.0 703.8 jit_solution(5103127675943364345)
XLA Ops:
  12.2 40.8 %all-reduce.15 = (f32[1024]{0:T(1024)S(1)}, f32[1024]{0:T(1024)S(1)}, f32[1024]{0:T(1024)S(1)}, f32[1024]{0:T(1024)S(1)}, f32[1024]{0:T(1024)S(1)}) all-reduce(f32[1024]{0:T(1024)S(1)} %dynamic-update-slice.4, f32[1024]{0:T(1024)S(1)} %dynamic-update-slice.3, ...), channel_id=1, replica_groups=mesh['dp'=8,'tensor'=4] {'dp','tensor'}, use_global_device_ids=true, to_apply=%add.4 | all-reduce | flops 5120 | bytes 40960
  54.2 1.3 fusion.63
  55.5 2.1 fusion.58
  57.8 10.8 %all-gather = bf16[8,2,32]{2,1,0:T(2,128)(2,1)S(1)} all-gather(bf16[1,2,32]{2,1,0:T(2,128)(2,1)} %bitcast.220), channel_id=1, replica_groups=mesh['dp'=8,'tensor'=4] {'dp'}, dimensions={0}, use_global_device_ids=true | all-gather | bytes 1152 | tf_op jit(solution)/shard_map/all_gather | solution.py:217
  68.9 9.6 %all_gather.53 = bf16[256,1024]{1,0:T(8,128)(2,1)S(1)} all-gather(bf16[256,128]{1,0:T(8,128)(2,1)} %param.25), channel_id=1, replica_groups=mesh['dp'=8,'tensor'=4] {'dp'}, dimensions={1}, use_global_device_ids=true | all-gather | bytes 589824 | tf_op jit(solution)/shard_map/all_gather | solution.py:218
  78.5 25.5 %all-gather.10.cloned.1.call-done = bf16[1024,1024]{1,0:T(8,128)(2,1)} async-done(((bf16[256,1024]{1,0:T(8,128)(2,1)}), bf16[1024,1024]{1,0:T(8,128)(2,1)}) %all-gather.10.cloned.1.call-update) | async-done | bytes 2097168 | tf_op jit(solution)/shard_map/all_gather | solution.py:48
  104.0 3.9 fusion.75
  108.6 19.6 %while.30 = (s32[]{:T(128)}, bf16[2,512,4,64]{1,3,2,0:T(8,128)(2,1)S(1)}, f32[2,4,512,1]{2,1,3,0:T(4,128)S(1)}, s32[2]{0:T(128)S(1)}, s32[1,4]{1,0:T(1,128)S(1)}...) while((s32[]{:T(128)}, ...), condition=%wide.region_6.7_spmd, body=%wide.region_2.6_spmd.sunk | while | flops 562186240 | bytes 30494096 | solution.py:134
  112.1 1.7 fusion.114
  113.8 2.3 exponential_reduce_fusion.2
  116.1 2.2 fusion.115
  121.9 1.7 fusion.114
  123.6 2.3 exponential_reduce_fusion.2
  125.9 2.2 fusion.115
  129.6 2.2 convolution_convert_fusion.4
  132.4 41.8 %reduce-scatter.15.cloned.1.call-done = bf16[256,1024]{1,0:T(8,128)(2,1)} async-done(((bf16[1024,1024]{1,0:T(8,128)(2,1)}), bf16[256,1024]{1,0:T(8,128)(2,1)}) %reduce-scatter.15.cloned.1.call-update) | async-done | bytes 524304 | tf_op jit(solution)/shard_map/reduce_scatter | solution.py:60
  175.5 1.4 multiply_reduce_fusion.1
  176.9 2.1 add_convert_fusion.1
  180.5 10.2 %all-gather.1 = bf16[8,2,64]{2,1,0:T(2,128)(2,1)S(1)} all-gather(bf16[1,2,64]{2,1,0:T(2,128)(2,1)S(1)} %bitcast.221), channel_id=1, replica_groups=mesh['dp'=8,'tensor'=4] {'dp'}, dimensions={0}, use_global_device_ids=true | all-gather | bytes 2304 | tf_op jit(solution)/shard_map/all_gather | solution.py:222
  190.8 13.0 %all-gather.16.cloned.1.call-done = bf16[1024,1024]{1,0:T(8,128)(2,1)} async-done(((bf16[128,1024]{1,0:T(8,128)(2,1)}), bf16[1024,1024]{1,0:T(8,128)(2,1)}) %all-gather.16.cloned.1.call-update) | async-done | bytes 2097168 | tf_op jit(solution)/shard_map/all_gather | solution.py:221
  203.8 47.1 %all-gather.14.cloned.1.call-done = bf16[1024,1024]{1,0:T(8,128)(2,1)} async-done(((bf16[256,1024]{1,0:T(8,128)(2,1)}), bf16[1024,1024]{1,0:T(8,128)(2,1)}) %all-gather.14.cloned.1.call-update) | async-done | bytes 2097168 | tf_op jit(solution)/shard_map/all_gather | solution.py:48
  250.9 6.5 fusion.76
  257.4 39.4 %all-gather.20.cloned.1.call-done = bf16[1024,1024]{1,0:T(8,128)(2,1)} async-done(((bf16[256,1024]{1,0:T(8,128)(2,1)}), bf16[1024,1024]{1,0:T(8,128)(2,1)}) %all-gather.20.cloned.1.call-update) | async-done | bytes 2097168 | tf_op jit(solution)/shard_map/all_gather | solution.py:52
  296.8 29.4 %all-gather.18.cloned.1.call-done = bf16[1024,1024]{1,0:T(8,128)(2,1)} async-done(((bf16[1024,128]{1,0:T(8,128)(2,1)}), bf16[1024,1024]{1,0:T(8,128)(2,1)}) %all-gather.18.cloned.1.call-update) | async-done | bytes 2097168 | tf_op jit(solution)/shard_map/all_gather | solution.py:223
  326.2 9.6 %fusion.71 = (bf16[1024]{0:T(1024)(128)(2,1)}, bf16[1024,1024]{1,0:T(8,128)(2,1)S(1)}) fusion(f32[1024,1024]{1,0:T(8,128)} %fusion.76, f32[1024]{0:T(1024)S(1)} %reshape.318, bf16[1024,1024]{1,0:T(8,128)(2,1)} %all-gather.20.cloned.1.call-done, bf16[1024,1024]{1,0:T(8,128)(2,1)} %all-gather.18.cloned.1.call-done), kind=kOutput, calls=%fused_computation.142 | convolution fusion | flops 2174745600 | bytes 10491904 | tf_op jit(solution)/shard_map/dot_general | solution.py:36
  335.8 1.3 copy-done.26
  337.1 3.7 convolution_convert_fusion.2
  340.9 42.9 %reduce-scatter.19.cloned.1.call-done = bf16[256,1024]{1,0:T(8,128)(2,1)} async-done(((bf16[1024,1024]{1,0:T(8,128)(2,1)}), bf16[256,1024]{1,0:T(8,128)(2,1)}) %reduce-scatter.19.cloned.1.call-update) | async-done | bytes 524304 | tf_op jit(solution)/shard_map/reduce_scatter | solution.py:73
  383.8 1.7 fusion.68
  385.5 1.7 fusion.73
  389.3 7.2 %convolution_convert_fusion = bf16[1024,1024]{1,0:T(8,128)(2,1)} fusion(bf16[1024,1024]{1,0:T(8,128)(2,1)} %all-gather.20.cloned.1.call-done, f32[1024,1024]{1,0:T(8,128)} %fusion.76, f32[1024]{0:T(1024)S(1)} %reshape.318), kind=kOutput, calls=%fused_computation.82 | convolution fusion | flops 2159017984 | bytes 8392704 | tf_op jit(solution)/shard_map/dot_general | solution.py:42
  396.5 4.0 copy.63
  400.6 6.0 convolution_convert_fusion.1
  406.7 27.6 %all-gather.22.cloned.1.call-done = bf16[1024,1024]{1,0:T(8,128)(2,1)} async-done(((bf16[256,1024]{1,0:T(8,128)(2,1)}), bf16[1024,1024]{1,0:T(8,128)(2,1)}) %all-gather.22.cloned.1.call-update) | async-done | bytes 2097168 | tf_op jit(solution)/shard_map/all_gather | solution.py:52
  434.3 3.1 convolution_convert_fusion.7
  437.4 2.0 copy.60
  439.7 3.1 convolution_convert_fusion.8
  444.1 56.9 %while.31 = (s32[]{:T(128)}, f32[1,1024,4,64]{1,3,2,0:T(8,128)S(1)}, f32[1,1024,4,64]{1,3,2,0:T(8,128)}, bf16[2,512,4,64]{1,0,3,2:T(2,128)(2,1)}, s32[2]{0:T(128...) while((s32[]{:T(128)}, ...), condition=%wide.region_17.18_spmd, body=%wide.region_14.17_spmd.sunk | while | flops 1376798720 | bytes 76885448 | solution.py:183
  448.9 4.5 fusion.123
  453.4 3.2 multiply_reduce_fusion.3
  456.6 2.4 multiply_convert_fusion.5
  459.0 1.4 fusion.124
  462.5 9.9 %dynamic_update_slice.31 = bf16[2,512,4,64]{1,0,3,2:T(2,128)(2,1)} dynamic-update-slice(bf16[2,512,4,64]{1,0,3,2:T(2,128)(2,1)} %get-tuple-element.503, bf16[1,512,4,64]{1,0,3,2:T(2,128)(2,1)} %copy.86, s32[]{:T(128)S(6)} %copy.108, s32[]{:T(128)} %constant.208.clone.1..sunk.1, s32[]{:T(128)} %constant.208.clone.1..sunk.1, s32[]{:T(128)} %constant.208.clone.1..sunk.1) | dynamic-update-slice | bytes 524292 | tf_op jit(solution)/shard_map/while/body/jit(dynamic_update_index_in_dim)/dynamic_update_slice | solution.py:183
  477.2 4.5 fusion.123
  481.7 3.2 multiply_reduce_fusion.3
  484.9 2.4 multiply_convert_fusion.5
  487.2 1.4 fusion.124
  490.8 9.9 %dynamic_update_slice.31 = bf16[2,512,4,64]{1,0,3,2:T(2,128)(2,1)} dynamic-update-slice(bf16[2,512,4,64]{1,0,3,2:T(2,128)(2,1)} %get-tuple-element.503, bf16[1,512,4,64]{1,0,3,2:T(2,128)(2,1)} %copy.86, s32[]{:T(128)S(6)} %copy.108, s32[]{:T(128)} %constant.208.clone.1..sunk.1, s32[]{:T(128)} %constant.208.clone.1..sunk.1, s32[]{:T(128)} %constant.208.clone.1..sunk.1) | dynamic-update-slice | bytes 524292 | tf_op jit(solution)/shard_map/while/body/jit(dynamic_update_index_in_dim)/dynamic_update_slice | solution.py:183
  500.9 2.2 stack_reshape.9
  503.1 1.8 maximum_convert_fusion
  505.1 1.3 copy-done.12
  506.5 3.0 convolution_convert_fusion.6
  509.6 5.1 convolution_convert_fusion.5
  514.8 7.2 %convolution_convert_fusion.3 = bf16[1024,1024]{1,0:T(8,128)(2,1)} fusion(bf16[1024,1024]{1,0:T(8,128)(2,1)} %all-gather.18.cloned.1.call-done, f32[1024,1024]{1,0:T(8,128)} %fusion.76, f32[1024]{0:T(1024)S(1)} %reshape.318), kind=kOutput, calls=%fused_computation.85 | convolution fusion | flops 2159017984 | bytes 8392704 | tf_op jit(solution)/shard_map/dot_general | solution.py:58
  525.6 1.8 convert_element_type.168
  527.4 1.4 slice_reduce_fusion
  528.9 21.5 %all-reduce.16 = (bf16[32,16]{1,0:T(8,128)(2,1)S(1)}, bf16[64,16]{1,0:T(8,128)(2,1)S(1)}) all-reduce(bf16[32,16]{1,0:T(8,128)(2,1)S(1)} %convert_element_type.163, bf16[64,16]{1,0:T(8,128)(2,1)S(1)} %convert_element_type.169), channel_id=9, replica_groups=mesh['dp'=8,'tensor'=4] {'dp'}, use_global_device_ids=true, to_apply=%region_27.28.clone | all-reduce | flops 1536 | bytes 6144
  551.8 7.3 %reduce-scatter.27.cloned.1.call-done = bf16[128,256]{1,0:T(8,128)(2,1)} async-done(((bf16[1024,256]{1,0:T(8,128)(2,1)}), bf16[128,256]{1,0:T(8,128)(2,1)}) %reduce-scatter.27.cloned.1.call-update) | async-done | bytes 65552
  560.8 40.4 %reduce-scatter.23.cloned.1.call-done = bf16[128,768]{1,0:T(8,128)(2,1)} async-done(((bf16[1024,768]{1,0:T(8,128)(2,1)}), bf16[128,768]{1,0:T(8,128)(2,1)}) %reduce-scatter.23.cloned.1.call-update) | async-done | bytes 196624 | tf_op jit(solution)/shard_map/reduce_scatter | solution.py:299
  601.2 1.7 convert_element_type.162
  602.9 43.9 %reduce-scatter.21.cloned.1.call-done = bf16[256,1024]{1,0:T(8,128)(2,1)} async-done(((bf16[1024,1024]{1,0:T(8,128)(2,1)}), bf16[256,1024]{1,0:T(8,128)(2,1)}) %reduce-scatter.21.cloned.1.call-update) | async-done | bytes 524304 | tf_op jit(solution)/shard_map/reduce_scatter | solution.py:73
  646.8 1.6 fusion.69
  648.4 42.3 %all-reduce.14 = (f32[1024]{0:T(1024)S(1)}, f32[1024]{0:T(1024)S(1)}, f32[1024]{0:T(1024)S(1)}, f32[1024]{0:T(1024)S(1)}, f32[1024]{0:T(1024)S(1)}, /*index=5*/f32[1024]{0:T(1024)S(1)}, f32[1024]{0:T(1024)S(1)}) all-reduce(f32[1024]{0:T(1024)S(1)} %dynamic-update-slice.5, ...), channel_id=1, replica_groups=mesh['dp'=8,'tensor'=4] {'dp','tensor'}, use_global_device_ids=true, to_apply=%add.5 | all-reduce | flops 7168 | bytes 57344
  694.3 2.7 fusion.62
  (185 shorter events, 38.5 us)
Async XLA Ops:
  7.2 71.4 %all-gather.12.cloned.1.call-start = ((), (), s32[]{:S(2)}) async-start(), calls=%async_computation.9 | async-start | bytes 1769472 | tf_op jit(solution)/shard_map/all_gather | solution.py:216
  7.9 96.1 %all-gather.10.cloned.1.call-start = ((), (), s32[]{:S(2)}) async-start(), calls=%async_computation.8 | async-start | bytes 2621440 | tf_op jit(solution)/shard_map/all_gather | solution.py:48
  53.0 4.7 copy-start.14
  54.2 3.5 copy-start.16
  55.5 2.2 copy-start.18
  57.7 116.5 %reduce-scatter.15.cloned.1.call-start = ((), (), s32[]{:S(2)}) async-start(), calls=%async_computation.10 | async-start | bytes 2621440 | tf_op jit(solution)/shard_map/reduce_scatter | solution.py:60
  78.5 50.3 %copy-start.8 = (bf16[256,1024]{1,0:T(8,128)(2,1)}, bf16[256,1024]{1,0:T(8,128)(2,1)S(1)}, u32[]{:S(2)}) copy-start(bf16[256,1024]{1,0:T(8,128)(2,1)S(1)} %all_gather.53) | copy-start | bytes 1572868
  107.9 0.7 copy-start.13
  128.2 46.0 %copy-start = (bf16[256,1024]{1,0:T(8,128)(2,1)S(1)}, bf16[256,1024]{1,0:T(8,128)(2,1)}, u32[]{:S(2)}) copy-start(bf16[256,1024]{1,0:T(8,128)(2,1)} %param.19) | copy-start | bytes 1572868
  128.8 0.8 copy-start.10
  131.8 48.7 %copy-start.21 = (bf16[64,2]{0,1:T(2,128)(2,1)S(1)}, bf16[64,2]{0,1:T(2,128)(2,1)}, u32[]{:S(2)}) copy-start(bf16[64,2]{0,1:T(2,128)(2,1)} %param.30) | copy-start | bytes 772
  131.8 72.0 %all-gather.16.cloned.1.call-start = ((), (), s32[]{:S(2)}) async-start(), calls=%async_computation.12 | async-start | bytes 2359296 | tf_op jit(solution)/shard_map/all_gather | solution.py:221
  132.4 118.5 %all-gather.14.cloned.1.call-start = ((), (), s32[]{:S(2)}) async-start(), calls=%async_computation.11 | async-start | bytes 2621440 | tf_op jit(solution)/shard_map/all_gather | solution.py:48
  179.1 117.7 %all-gather.20.cloned.1.call-start = ((), (), s32[]{:S(2)}) async-start(), calls=%async_computation.15 | async-start | bytes 2621440 | tf_op jit(solution)/shard_map/all_gather | solution.py:52
  179.7 146.5 %all-gather.18.cloned.1.call-start = ((), (), s32[]{:S(2)}) async-start(), calls=%async_computation.13 | async-start | bytes 2359296 | tf_op jit(solution)/shard_map/all_gather | solution.py:223
  180.4 203.4 %reduce-scatter.19.cloned.1.call-start = ((), (), s32[]{:S(2)}) async-start(), calls=%async_computation.16 | async-start | bytes 2621440 | tf_op jit(solution)/shard_map/reduce_scatter | solution.py:73
  326.2 10.9 %copy-start.23 = (bf16[1024,1024]{1,0:T(8,128)(2,1)S(1)}, bf16[1024,1024]{1,0:T(8,128)(2,1)}, u32[]{:S(2)}) copy-start(bf16[1024,1024]{1,0:T(8,128)(2,1)} %all-gather.16.cloned.1.call-done) | copy-start | bytes 6291460
  335.8 1.3 copy-start.26
  337.1 46.7 %copy-start.1 = (bf16[256,1024]{1,0:T(8,128)(2,1)S(1)}, bf16[256,1024]{1,0:T(8,128)(2,1)}, u32[]{:S(2)}) copy-start(bf16[256,1024]{1,0:T(8,128)(2,1)} %reduce-scatter.15.cloned.1.call-done) | copy-start | bytes 1572868
  337.1 48.4 %copy-start.7 = (bf16[256,1024]{1,0:T(8,128)(2,1)S(1)}, bf16[256,1024]{1,0:T(8,128)(2,1)}, u32[]{:S(2)}) copy-start(bf16[256,1024]{1,0:T(8,128)(2,1)} %param.33) | copy-start | bytes 1572868
  340.8 93.5 %all-gather.22.cloned.1.call-start = ((), (), s32[]{:S(2)}) async-start(), calls=%async_computation.17 | async-start | bytes 2621440 | tf_op jit(solution)/shard_map/all_gather | solution.py:52
  387.2 1.0 copy-start.4
  389.0 134.6 %reduce-scatter.29.cloned.1.call-start = ((), (), s32[]{:S(2)}) async-start(), calls=%async_computation.22 | async-start | bytes 2359296
  400.5 33.8 %copy-start.11 = (bf16[32,8,2,512]{3,1,2,0:T(8,128)(2,1)S(1)}, bf16[32,8,2,512]{3,1,2,0:T(8,128)(2,1)}, u32[]{:S(2)}) copy-start(bf16[32,8,2,512]{3,1,2,0:T(8,128)(2,1)} %copy-done.10) | copy-start | bytes 1572868
  400.5 125.1 %reduce-scatter.25.cloned.1.call-start = ((), (), s32[]{:S(2)}) async-start(), calls=%async_computation.20 | async-start | bytes 2359296 | tf_op jit(solution)/shard_map/reduce_scatter | solution.py:264
  406.6 33.1 %copy-start.9 = (bf16[256,1024]{1,0:T(8,128)(2,1)S(1)}, bf16[256,1024]{1,0:T(8,128)(2,1)}, u32[]{:S(2)}) copy-start(bf16[256,1024]{1,0:T(8,128)(2,1)} %copy-done.8) | copy-start | bytes 1572868
  406.6 152.5 %reduce-scatter.27.cloned.1.call-start = ((), (), s32[]{:S(2)}) async-start(), calls=%async_computation.21 | async-start | bytes 589824
  439.5 161.7 %reduce-scatter.23.cloned.1.call-start = ((), (), s32[]{:S(2)}) async-start(), calls=%async_computation.19 | async-start | bytes 1769472 | tf_op jit(solution)/shard_map/reduce_scatter | solution.py:299
  447.6 1.3 copy-start.6
  475.9 1.3 copy-start.6
  503.1 3.3 copy-start.22
  505.0 4.5 copy-start.3
  505.1 1.3 copy-start.12
  509.5 137.3 %reduce-scatter.21.cloned.1.call-start = ((), (), s32[]{:S(2)}) async-start(), calls=%async_computation.18 | async-start | bytes 2621440 | tf_op jit(solution)/shard_map/reduce_scatter | solution.py:73
  514.7 7.3 %copy-start.25 = (u32[32]{0:T(128)S(1)}, u32[32]{0:T(128)}, u32[]{:S(2)}) copy-start(u32[32]{0:T(128)} %constant.252) | copy-start | bytes 388
  514.7 8.6 %copy-start.24 = (f32[32]{0:T(128)S(1)}, f32[32]{0:T(128)}, u32[]{:S(2)}) copy-start(f32[32]{0:T(128)} %param.32) | copy-start | bytes 388
  514.7 8.8 %copy-start.20 = (bf16[1024]{0:T(1024)(128)(2,1)S(1)}, bf16[1024]{0:T(1024)(128)(2,1)}, u32[]{:S(2)}) copy-start(bf16[1024]{0:T(1024)(128)(2,1)} %get-tuple-element.314) | copy-start | bytes 6148
  514.7 179.5 %reduce-scatter.17.cloned.1.call-start = ((), (), s32[]{:S(2)}) async-start(), calls=%async_computation.14 | async-start | bytes 2621440 | tf_op jit(solution)/shard_map/reduce_scatter | solution.py:60
  522.0 124.8 %copy-start.15 = (f32[1024]{0:T(1024)S(1)}, f32[1024]{0:T(1024)}, u32[]{:S(2)}) copy-start(f32[1024]{0:T(1024)} %copy-done.14) | copy-start | bytes 12292
  522.0 124.8 %copy-start.17 = (f32[256]{0:T(256)S(1)}, f32[256]{0:T(256)}, u32[]{:S(2)}) copy-start(f32[256]{0:T(256)} %copy-done.16) | copy-start | bytes 3076
  522.0 124.8 %copy-start.19 = (f32[256]{0:T(256)S(1)}, f32[256]{0:T(256)}, u32[]{:S(2)}) copy-start(f32[256]{0:T(256)} %copy-done.18) | copy-start | bytes 3076
  522.0 172.3 %copy-start.2 = (bf16[256,1024]{1,0:T(8,128)(2,1)S(1)}, bf16[256,1024]{1,0:T(8,128)(2,1)}, u32[]{:S(2)}) copy-start(bf16[256,1024]{1,0:T(8,128)(2,1)} %reduce-scatter.15.cloned.1.call-done) | copy-start | bytes 1572868
  522.0 172.3 %copy-start.5 = (f32[256,1024]{1,0:T(8,128)S(1)}, f32[256,1024]{1,0:T(8,128)}, u32[]{:S(2)}) copy-start(f32[256,1024]{1,0:T(8,128)} %copy-done.4) | copy-start | bytes 3145732
Sparse Core Ops, SparseCore 0:
  9.9 28.1 all-gather.11
  57.8 46.1 all-gather.9
  131.9 42.2 reduce-scatter.14
  176.0 27.7 all-gather.15
  205.8 45.0 all-gather.13
  252.3 44.4 all-gather.19
  298.7 27.4 all-gather.17
  341.0 42.7 reduce-scatter.18
  389.2 45.0 all-gather.21
  437.4 39.9 reduce-scatter.28
  480.7 41.1 reduce-scatter.24
  525.3 33.7 reduce-scatter.26
  562.4 38.6 reduce-scatter.22
  603.3 43.4 reduce-scatter.20
  648.9 43.9 reduce-scatter.16
where the time goes:
time: 712 us; the launch traced here: 704 us
  waiting for transfers between devices  361 us (51%)
  blocking collectives  135 us (19%)
  matrix products  91.2 us (13%)
  local copies, waits for them, and re-layouts  52.4 us (7%)
  other arithmetic  39.5 us (6%)
  between operations  15.3 us (2%)
  loops' own time  8.35 us (1%)
    unnamed x3, blocking collectives  105 us
    reduce_scatter x2, waiting for transfers between devices, reduce_grads(): lax.psum_scatter(term(jnp.int32(0), lax.axis_size('tensor') * rows).astyp...  86.8 us
    all_gather x2, waiting for transfers between devices, gather_rows(): return lax.all_gather(values, 'tensor', axis=0, tiled=True)  72.6 us
    all_gather x2, waiting for transfers between devices, gather_grads(): return lax.all_gather(values, 'tensor', axis=0, tiled=True)  67 us
    reduce_scatter x2, waiting for transfers between devices, reduce_rows(): lax.psum_scatter(term(jnp.int32(0), lax.axis_size('tensor') * rows).astyp...  41.8 us
    reduce_scatter x1, waiting for transfers between devices, per_device(): lax.psum_scatter(grad_w_qkv.astype(jnp.bfloat16), 'dp', scatter_dimension...  40.4 us
    all_gather x1, waiting for transfers between devices, per_device(): lax.all_gather(w_down, 'dp', axis=1, tiled=True)  29.4 us
    unnamed x78, local copies, waits for them, and re-layouts  22.9 us
  transfers between devices with their start and end apart: 15, of which 11 were waited for; matrix products, arithmetic and copies ran while one was open for 19% of the time, Pallas kernels for 0%

commit v1 on v0

--- a/solution.py
+++ b/solution.py
@@ -1,6 +1,10 @@
+import functools
+
 import jax
 import jax.numpy as jnp
 from jax import lax
+from jax.experimental import pallas as pl
+from jax.experimental.pallas import tpu as pltpu
 from jax.sharding import PartitionSpec as P
 
 HD = 64
@@ -337,9 +341,852 @@
     )
 
 
+MESH = pl.DeviceIdType.MESH
+CH = 2
+
+
+class Fused:
+    def __init__(self, names, refs):
+        for name, ref in zip(names, refs):
+            setattr(self, name, ref)
+        self.next_sem = 0
+        self.unsent = []
+        self.groups = {0: [], 1: []}
+        dp, self.z = lax.axis_index("dp"), lax.axis_index("tensor")
+        self.y, self.x, self.c = dp // 4, (dp // 2) % 2, dp % 2
+        self.j = 2 * self.x + self.c
+        self.q = self.quarter(self.j)
+        self.sib = self.dev(self.y, self.x, 1 - self.c, self.z)
+        self.across = self.dev(self.y, 1 - self.x, self.c, self.z)
+        self.q_sib = self.quarter(2 * self.x + 1 - self.c)
+        self.q_x = self.quarter(2 * (1 - self.x) + self.c)
+        self.q_d = self.quarter(2 * (1 - self.x) + 1 - self.c)
+        self.rows = self.tok.shape[0]
+        self.width = self.tok.shape[1]
+        self.part = self.width // 8
+
+    def dev(self, y, x, c, z):
+        return ((y * 2 + x) * 2 + c, z)
+
+    def quarter(self, member):
+        return (member - self.z + 4) % 4
+
+    def sem(self):
+        index = self.next_sem
+        self.next_sem += 1
+        return index
+
+    def copy(self, src, dst, device, index):
+        return pltpu.make_async_remote_copy(
+            src_ref=src,
+            dst_ref=dst,
+            send_sem=self.ssem.at[index],
+            recv_sem=self.rsem.at[index],
+            device_id=device,
+            device_id_type=MESH,
+        )
+
+    def send(self, src, dst, device, index, group=None):
+        copy = self.copy(src, dst, device, index)
+        copy.start()
+        (self.unsent if group is None else self.groups[group]).append(copy)
+
+    def arrived(self, dst, index):
+        self.copy(dst, dst, self.sib, index).wait_recv()
+
+    def drain(self):
+        for copy in self.unsent + self.groups[0] + self.groups[1]:
+            copy.wait_send()
+
+    def at_quarter(self, quarter, chunk=None):
+        if chunk is None:
+            return pl.ds(pl.multiple_of(quarter * self.rows, self.rows), self.rows)
+        size = self.rows // CH
+        return pl.ds(pl.multiple_of(quarter * self.rows + chunk * size, size), size)
+
+    def at_chunk(self, chunk):
+        size = self.rows // CH
+        return pl.ds(chunk * size, size)
+
+    def barrier(self):
+        me = lax.axis_index("dp") * 4 + self.z
+        bar = pltpu.get_barrier_semaphore()
+
+        def greet(step, carry):
+            other = (me + step) % 32
+            pl.semaphore_signal(
+                bar, inc=1, device_id=(other // 4, other % 4), device_id_type=MESH
+            )
+            return carry
+
+        lax.fori_loop(1, 32, greet, 0)
+        pl.semaphore_wait(bar, 31)
+
+    def homes(self):
+        plane = 2 * self.y + self.x
+        member = (plane + self.z) % 4
+        worker = (self.c, member // 2, member % 2, plane)
+        owner = (self.z // 2, self.z % 2, self.y, self.q)
+        same = (
+            (worker[0] == self.y)
+            & (worker[1] == self.x)
+            & (worker[2] == self.c)
+            & (worker[3] == self.z)
+        )
+        return self.dev(*worker), self.dev(*owner), same
+
+    def move_start(self, src, dst, outward, index):
+        worker, owner, same = self.homes()
+        copy = self.copy(src, dst, worker if outward else owner, index)
+        local = pltpu.make_async_copy(src, dst, self.lsem.at[index])
+
+        @pl.when(jnp.logical_not(same))
+        def _():
+            copy.start()
+
+        @pl.when(same)
+        def _():
+            local.start()
+
+    def move_wait(self, src, dst, index):
+        same = self.homes()[2]
+        copy = self.copy(src, dst, self.sib, index)
+        local = pltpu.make_async_copy(src, dst, self.lsem.at[index])
+
+        @pl.when(jnp.logical_not(same))
+        def _():
+            copy.wait_send()
+            copy.wait_recv()
+
+        @pl.when(same)
+        def _():
+            local.wait()
+
+    def span(self, half):
+        return pl.ds(pl.multiple_of(half * 4 * self.part, 4 * self.part), 4 * self.part)
+
+    def place(self, source):
+        return pl.ds(pl.multiple_of(source * self.part, self.part), self.part)
+
+    def cut(self, kind, ref, zc, where):
+        if kind == "q":
+            return ref.at[:, zc, :, where]
+        if kind == "u":
+            return ref.at[zc, where, :]
+        return ref.at[zc, :, where]
+
+    def piece(self, kind, ref, member):
+        if kind == "u":
+            wide = self.wbuf["u"].shape[2]
+            return ref.at[:, pl.ds(pl.multiple_of(member * wide, wide), wide)]
+        return ref.at[member]
+
+    def weights_one(self, kind):
+        source = self.dev(self.y, self.x, self.c, self.z)[0]
+        here = self.cut(kind, self.wbuf[kind], self.z, self.place(source))
+        self.one[kind] = []
+        for step in range(1, 4):
+            member = (self.j + step) % 4
+            index = self.sem()
+            self.send(
+                self.piece(kind, self.shard[kind], member),
+                here,
+                self.dev(self.y, member // 2, member % 2, self.z),
+                index,
+            )
+            sender = self.y * 4 + (self.j - step + 4) % 4
+            self.one[kind].append(
+                (self.cut(kind, self.wbuf[kind], self.z, self.place(sender)), index)
+            )
+        index = self.sem()
+        local = pltpu.make_async_copy(
+            self.piece(kind, self.shard[kind], self.j), here, self.lsem.at[index]
+        )
+        local.start()
+        self.own[kind] = local
+
+    def weights_two(self, kind):
+        self.own[kind].wait()
+        for view, index in self.one[kind]:
+            self.arrived(view, index)
+        mine = self.cut(kind, self.wbuf[kind], self.z, self.span(self.y))
+        self.two[kind] = []
+        for step in range(1, 4):
+            plane = (self.z + step) % 4
+            index = self.sem()
+            self.send(mine, mine, self.dev(self.y, self.x, self.c, plane), index)
+            self.two[kind].append(((self.z - step + 4) % 4, index))
+        self.three[kind] = []
+        self.weights_cross(kind, self.z)
+
+    def weights_cross(self, kind, plane):
+        index = self.sem()
+        mine = self.cut(kind, self.wbuf[kind], plane, self.span(self.y))
+        self.send(mine, mine, self.dev(1 - self.y, self.x, self.c, self.z), index)
+        self.three[kind].append((plane, index))
+
+    def weights_three(self, kind):
+        for plane, index in self.two[kind]:
+            self.arrived(self.cut(kind, self.wbuf[kind], plane, self.span(self.y)), index)
+            self.weights_cross(kind, plane)
+
+    def weights_done(self, kind):
+        for plane, index in self.three[kind]:
+            self.arrived(self.cut(kind, self.wbuf[kind], plane, self.span(1 - self.y)), index)
+
+    def grads_one(self, kind):
+        index = self.sem()
+        self.back[kind] = index
+        for plane in range(4):
+            away = self.cut(kind, self.dbuf[kind], plane, self.span(1 - self.y))
+            there = self.cut(kind, self.ybuf[kind], plane, slice(None))
+            use = index if plane == 0 else self.sem()
+            self.send(away, there, self.dev(1 - self.y, self.x, self.c, self.z), use)
+            self.backs.setdefault(kind, []).append(use)
+
+    def grads_two(self, kind):
+        for plane in range(4):
+            there = self.cut(kind, self.ybuf[kind], plane, slice(None))
+            self.arrived(there, self.backs[kind][plane])
+            mine = self.cut(kind, self.dbuf[kind], plane, self.span(self.y))
+            mine[...] = (
+                mine[...].astype(jnp.float32) + there[...].astype(jnp.float32)
+            ).astype(jnp.bfloat16)
+        self.swaps[kind] = []
+        for step in range(1, 4):
+            plane = (self.z + step) % 4
+            index = self.sem()
+            self.send(
+                self.cut(kind, self.dbuf[kind], plane, self.span(self.y)),
+                self.zbuf[kind].at[step - 1],
+                self.dev(self.y, self.x, self.c, plane),
+                index,
+            )
+            self.swaps[kind].append(index)
+
+    def grads_three(self, kind):
+        mine = self.cut(kind, self.dbuf[kind], self.z, self.span(self.y))
+        total = mine[...].astype(jnp.float32)
+        for step in range(1, 4):
+            there = self.zbuf[kind].at[step - 1]
+            self.arrived(there, self.swaps[kind][step - 1])
+            total = total + there[...].astype(jnp.float32)
+        final = self.fbuf[kind]
+        final[...] = total.astype(jnp.bfloat16)
+        ends = self.ebuf[kind]
+        self.last[kind] = []
+        for step in range(1, 4):
+            member = (self.j + step) % 4
+            index = self.sem()
+            self.send(
+                self.slab(kind, final, member),
+                ends.at[self.j],
+                self.dev(self.y, member // 2, member % 2, self.z),
+                index,
+            )
+            self.last[kind].append(((self.j - step + 4) % 4, index))
+        index = self.sem()
+        local = pltpu.make_async_copy(
+            self.slab(kind, final, self.j), ends.at[self.j], self.lsem.at[index]
+        )
+        local.start()
+        self.own[kind] = local
+
+    def slab(self, kind, ref, member):
+        where = pl.ds(pl.multiple_of(member * self.part, self.part), self.part)
+        if kind == "q":
+            return ref.at[:, :, where]
+        if kind == "u":
+            return ref.at[where, :]
+        return ref.at[:, where]
+
+    def grads_done(self, kind):
+        self.own[kind].wait()
+        for member, index in self.last[kind]:
+            self.arrived(self.ebuf[kind].at[member], index)
+
+    def gather_plan(self):
+        return {kind: [self.sem() for _ in range(CH)] for kind in ("across", "sib", "pass")}
+
+    def gather_send(self, buf, plan, chunk):
+        rows = self.at_quarter(self.q, chunk)
+        self.send(buf.at[rows], buf.at[rows], self.across, plan["across"][chunk])
+        self.send(buf.at[rows], buf.at[rows], self.sib, plan["sib"][chunk])
+
+    def gather_pass(self, buf, plan):
+        for chunk in range(CH):
+            rows = self.at_quarter(self.q_x, chunk)
+            self.arrived(buf.at[rows], plan["across"][chunk])
+            self.send(buf.at[rows], buf.at[rows], self.sib, plan["pass"][chunk])
+
+    def gather_sib(self, buf, plan):
+        for chunk in range(CH):
+            self.arrived(buf.at[self.at_quarter(self.q_sib, chunk)], plan["sib"][chunk])
+
+    def gather_last(self, buf, plan):
+        for chunk in range(CH):
+            self.arrived(buf.at[self.at_quarter(self.q_d, chunk)], plan["pass"][chunk])
+
+    def gathered(self, buf, plan, use):
+        use(self.q)
+        self.gather_sib(buf, plan)
+        use(self.q_sib)
+        self.gather_pass(buf, plan)
+        use(self.q_x)
+        self.gather_last(buf, plan)
+        use(self.q_d)
+
+    def scatter_start(self, partial, own, which, rx):
+        sa, ra, sb, sc, rb = (self.rs.at[which, slot] for slot in range(5))
+        plan = [[self.sem() for _ in range(CH)] for _ in range(3)]
+        low = jnp.bfloat16
+        for copy in self.groups[which]:
+            copy.wait_send()
+        self.groups[which] = []
+        sa[...] = partial(self.q_d).astype(low)
+        for chunk in range(CH):
+            rows = self.at_chunk(chunk)
+            self.send(sa.at[rows], ra.at[rows], self.sib, plan[0][chunk], which)
+        held = partial(self.q_x)
+        for chunk in range(CH):
+            self.arrived(ra.at[self.at_chunk(chunk)], plan[0][chunk])
+        sb[...] = (held + ra[...].astype(jnp.float32)).astype(low)
+        for chunk in range(CH):
+            rows = self.at_chunk(chunk)
+            self.send(sb.at[rows], rx.at[rows], self.across, plan[1][chunk], which)
+        sc[...] = partial(self.q_sib).astype(low)
+        for chunk in range(CH):
+            rows = self.at_chunk(chunk)
+            self.send(sc.at[rows], rb.at[rows], self.sib, plan[2][chunk], which)
+        own[...] = partial(self.q)
+        return plan, which, rx
+
+    def scatter_chunk(self, started, own, chunk):
+        plan, which, rx = started
+        rows = self.at_chunk(chunk)
+        rb = self.rs.at[which, 4]
+        self.arrived(rb.at[rows], plan[2][chunk])
+        self.arrived(rx.at[rows], plan[1][chunk])
+        return (
+            own[rows, :] + rb[rows, :].astype(jnp.float32) + rx[rows, :].astype(jnp.float32)
+        )
+
+    def run(self):
+        f32, low = jnp.float32, jnp.bfloat16
+        rows, width = self.rows, self.width
+        quarters = range(4)
+        self.wbuf = dict(q=self.wq, o=self.wo, u=self.wu, d=self.wd)
+        self.shard = dict(q=self.in_q, o=self.in_o, u=self.in_u, d=self.in_d)
+        self.dbuf = dict(q=self.dq, o=self.do, u=self.du, d=self.dd)
+        self.ybuf = dict(q=self.yq, o=self.yo, u=self.yu, d=self.yd)
+        self.zbuf = dict(q=self.zq, o=self.zo, u=self.zu, d=self.zd)
+        self.fbuf = dict(q=self.fq, o=self.fo, u=self.fu, d=self.fd)
+        self.ebuf = dict(q=self.eq, o=self.eo, u=self.eu, d=self.ed)
+        self.one, self.two, self.three, self.own = {}, {}, {}, {}
+        self.back, self.backs, self.swaps, self.last = {}, {}, {}, {}
+        gain_one, shift_one = self.small[0:1, :], self.small[1:2, :]
+        bias_out = self.small[2:3, :]
+        gain_two, shift_two = self.small[3:4, :], self.small[4:5, :]
+        bias_down = self.small[5:6, :]
+        heads, dim = self.qh.shape[0], self.qh.shape[2]
+        hidden = self.wu.shape[2]
+
+        self.barrier()
+        move = [self.sem() for _ in range(4)]
+        self.move_start(self.tok, self.xs, True, move[0])
+        for kind in "qoud":
+            self.weights_one(kind)
+        plan_one, plan_two, plan_go, plan_mid = (self.gather_plan() for _ in range(4))
+        self.weights_two("q")
+        self.move_wait(self.tok, self.xs, move[0])
+
+        for chunk in range(CH):
+            part = self.at_chunk(chunk)
+            normed, inverse = normalize(self.xs[part, :].astype(f32))
+            self.n1[part, :] = normed
+            self.i1[part, :] = inverse
+            self.h1[self.at_quarter(self.q, chunk), :] = (normed * gain_one + shift_one).astype(low)
+            self.gather_send(self.h1, plan_one, chunk)
+        for kind in "ou":
+            self.weights_two(kind)
+        self.move_start(self.go, self.gx, True, move[1])
+        self.weights_two("d")
+        self.mask_blocks()
+        self.weights_three("q")
+        self.gather_sib(self.h1, plan_one)
+        self.gather_pass(self.h1, plan_one)
+        self.weights_done("q")
+        self.gather_last(self.h1, plan_one)
+
+        def project(block, carry):
+            place = pl.ds(pl.multiple_of(block * rows, rows), rows)
+            weight = self.wq[...].reshape(3 * heads * dim, width)
+            both = dot_last(self.h1[place, :], weight) + self.bq[...]
+            for head in range(heads):
+                for slot, ref in enumerate((self.qh, self.kh, self.vh)):
+                    first = (slot * heads + head) * dim
+                    value = both[:, first : first + dim].astype(low)
+                    if slot == 0:
+                        value = (value.astype(f32) * 0.125).astype(low)
+                    ref[head, place, :] = value
+            return carry
+
+        lax.fori_loop(0, 4, project, 0)
+        self.weights_three("o")
+
+        def parts_of(block):
+            return ([(0, block * rows)] if block else []) + [(block * rows, rows)]
+
+        def attend(head, carry):
+            for block in quarters:
+                place = pl.ds(block * rows, rows)
+                query = self.qh[head, place, :]
+                scores = []
+                for first, count in parts_of(block):
+                    value = dot_last(query, self.kh[head, pl.ds(first, count), :])
+                    if first == block * rows:
+                        value = value + self.mk[block].astype(f32)
+                    scores.append(value)
+                peak = functools.reduce(
+                    jnp.maximum, [jnp.max(value, axis=1, keepdims=True) for value in scores]
+                )
+                powers = [jnp.exp(value - peak) for value in scores]
+                total = sum(jnp.sum(value, axis=1, keepdims=True) for value in powers)
+                scale = 1.0 / total
+                result = 0.0
+                for (first, count), value in zip(parts_of(block), powers):
+                    probs = (value * scale).astype(low)
+                    self.pb[block][head, :, pl.ds(first, count)] = probs
+                    result = result + jnp.dot(
+                        probs,
+                        self.vh[head, pl.ds(first, count), :],
+                        preferred_element_type=f32,
+                    )
+                self.hh[head, place, :] = result.astype(low)
+            return carry
+
+        lax.fori_loop(0, heads, attend, 0)
+
+        def assemble(target, refs, count):
+            def one(block, carry):
+                place = pl.ds(pl.multiple_of(block * rows, rows), rows)
+                pieces = [ref[head, place, :] for ref in refs for head in range(count)]
+                target[place, :] = jnp.concatenate(pieces, axis=1)
+                return carry
+
+            lax.fori_loop(0, 4, one, 0)
+
+        assemble(self.ho, (self.hh,), heads)
+        self.weights_done("o")
+        self.weights_three("u")
+
+        flat_out = lambda: self.wo[...].reshape(heads * dim, width)
+        started = self.scatter_start(
+            lambda quarter: jnp.dot(
+                self.ho[self.at_quarter(quarter), :], flat_out(), preferred_element_type=f32
+            ),
+            self.own_a,
+            0,
+            self.rx.at[0],
+        )
+        for chunk in range(CH):
+            part = self.at_chunk(chunk)
+            summed = self.scatter_chunk(started, self.own_a, chunk)
+            middle = self.xs[part, :].astype(f32) + (summed + bias_out)
+            self.mid[part, :] = middle
+            normed, inverse = normalize(middle)
+            self.n2[part, :] = normed
+            self.i2[part, :] = inverse
+            self.h2[self.at_quarter(self.q, chunk), :] = (normed * gain_two + shift_two).astype(low)
+            self.gather_send(self.h2, plan_two, chunk)
+        self.weights_three("d")
+        self.weights_done("u")
+
+        def up(quarter):
+            place = self.at_quarter(quarter)
+
+            for block in range(4):
+                lanes = pl.ds(block * hidden, hidden)
+                value = (
+                    jnp.dot(self.h2[place, :], self.wu[block], preferred_element_type=f32)
+                    + self.bu[:, lanes]
+                )
+                square = value * value
+                bend = jnp.tanh(ROOT * (value + 0.044715 * value * square))
+                self.hid[place, lanes] = (0.5 * value * (1.0 + bend)).astype(low)
+                slope = 0.5 * (1.0 + bend) + 0.5 * value * (1.0 - bend * bend) * ROOT * (
+                    1.0 + 3.0 * 0.044715 * square
+                )
+                self.gu[place, lanes] = slope.astype(low)
+
+        self.gathered(self.h2, plan_two, up)
+
+        self.move_wait(self.go, self.gx, move[1])
+        for chunk in range(CH):
+            part = self.at_chunk(chunk)
+            self.gg[self.at_quarter(self.q, chunk), :] = self.gx[part, :]
+            self.gather_send(self.gg, plan_go, chunk)
+        self.weights_done("d")
+        flat_down = lambda: self.wd[...].reshape(4 * hidden, width)
+        started_down = self.scatter_start(
+            lambda quarter: jnp.dot(
+                self.hid[self.at_quarter(quarter), :], flat_down(), preferred_element_type=f32
+            ),
+            self.own_b,
+            1,
+            self.rx.at[1],
+        )
+
+        def to_up(quarter):
+            place = self.at_quarter(quarter)
+            value = dot_last(self.gg[place, :], flat_down())
+            self.gu[place, :] = (self.gu[place, :].astype(f32) * value).astype(low)
+
+        self.gathered(self.gg, plan_go, to_up)
+        grad_out = self.gx[...].astype(f32)
+        self.sums[5:6, :] = jnp.sum(grad_out, axis=0, keepdims=True)
+
+        def two_part(quarter):
+            place = self.at_quarter(quarter)
+            return sum(
+                dot_last(self.gu[place, pl.ds(block * hidden, hidden)], self.wu[block])
+                for block in range(4)
+            )
+
+        started = self.scatter_start(two_part, self.own_a, 0, self.rx.at[0])
+
+        def down_grad(block, carry):
+            lanes = pl.ds(pl.multiple_of(block * hidden, hidden), hidden)
+            self.dd[block] = dot_first(self.hid[:, lanes], self.gg[...]).astype(low)
+            return carry
+
+        lax.fori_loop(0, 4, down_grad, 0)
+        self.grads_one("d")
+        step = width // 4
+
+        def up_grad(block, carry):
+            lanes = pl.ds(pl.multiple_of(block * step, step), step)
+            value = dot_first(self.h2[:, lanes], self.gu[...]).astype(low)
+            for plane in range(4):
+                self.du[plane, lanes, :] = value[:, plane * hidden : (plane + 1) * hidden]
+            return carry
+
+        lax.fori_loop(0, 4, up_grad, 0)
+        self.grads_one("u")
+        totals = [0.0] * 3
+        for chunk in range(CH):
+            part = self.at_chunk(chunk)
+            grad_two = self.scatter_chunk(started, self.own_a, chunk)
+            normed = self.n2[part, :]
+            middle = self.gx[part, :].astype(f32) + norm_back(
+                grad_two, normed, self.i2[part, :], gain_two
+            )
+            self.gm[part, :] = middle
+            self.ga[self.at_quarter(self.q, chunk), :] = middle.astype(low)
+            self.gather_send(self.ga, plan_mid, chunk)
+            for place, value in enumerate((grad_two * normed, grad_two, middle)):
+                totals[place] = totals[place] + jnp.sum(value, axis=0, keepdims=True)
+        self.sums[3:4, :] = totals[0]
+        self.sums[4:5, :] = totals[1]
+        self.sums[2:3, :] = totals[2]
+        self.bsum[0:1, :] = jnp.sum(self.gu[...].astype(f32), axis=0, keepdims=True)
+        for chunk in range(CH):
+            part = self.at_chunk(chunk)
+            summed = self.scatter_chunk(started_down, self.own_b, chunk)
+            self.ox[part, :] = (self.mid[part, :] + summed + bias_down).astype(low)
+        self.move_start(self.ox, self.out, False, move[2])
+        self.grads_two("d")
+
+        def to_heads(quarter):
+            place = self.at_quarter(quarter)
+            value = dot_last(self.ga[place, :], flat_out()).astype(low)
+            for head in range(heads):
+                self.hh[head, place, :] = value[:, head * dim : (head + 1) * dim]
+
+        self.gathered(self.ga, plan_mid, to_heads)
+        self.grads_two("u")
+        self.do[...] = dot_first(self.ho[...], self.ga[...]).astype(low).reshape(self.do.shape)
+        self.grads_one("o")
+
+        def attend_back(head, carry):
+            self.ka[...] = jnp.zeros_like(self.ka)
+            self.va[...] = jnp.zeros_like(self.va)
+            for block in quarters:
+                place = pl.ds(block * rows, rows)
+                query = self.qh[head, place, :]
+                grads = self.hh[head, place, :]
+                probs, values = [], []
+                inner = 0.0
+                for first, count in parts_of(block):
+                    span = pl.ds(first, count)
+                    prob = self.pb[block][head, :, span]
+                    value = dot_last(grads, self.vh[head, span, :])
+                    self.va[span, :] += dot_first(prob, grads)
+                    prob = prob.astype(f32)
+                    inner = inner + jnp.sum(prob * value, axis=1, keepdims=True)
+                    probs.append(prob)
+                    values.append(value)
+                result = 0.0
+                for (first, count), prob, value in zip(parts_of(block), probs, values):
+                    span = pl.ds(first, count)
+                    score = (prob * (value - inner)).astype(low)
+                    result = result + jnp.dot(
+                        score, self.kh[head, span, :], preferred_element_type=f32
+                    )
+                    self.ka[span, :] += dot_first(score, query)
+                self.qh[head, place, :] = (result * 0.125).astype(low)
+            self.kh[head] = self.ka[...].astype(low)
+            self.vh[head] = self.va[...].astype(low)
+            return carry
+
+        lax.fori_loop(0, heads, attend_back, 0)
+        assemble(self.gp, (self.qh, self.kh, self.vh), heads)
+        self.grads_three("d")
+        self.grads_three("u")
+
+        def project_grad(slot, carry):
+            lanes = pl.ds(pl.multiple_of(slot * heads * dim, heads * dim), heads * dim)
+            value = dot_first(self.gp[:, lanes], self.h1[...]).astype(low)
+            self.dq[slot] = value.reshape(heads, dim, width)
+            return carry
+
+        lax.fori_loop(0, 3, project_grad, 0)
+        self.grads_one("q")
+        self.grads_two("o")
+        started = self.scatter_start(
+            lambda quarter: jnp.dot(
+                self.gp[self.at_quarter(quarter), :],
+                self.wq[...].reshape(3 * heads * dim, width),
+                preferred_element_type=f32,
+            ),
+            self.own_b,
+            1,
+            self.rx.at[2],
+        )
+        self.bsum[1:2, : 3 * heads * dim] = jnp.sum(
+            self.gp[...].astype(f32), axis=0, keepdims=True
+        )
+        self.grads_two("q")
+        self.grads_three("o")
+        totals = [0.0] * 2
+        for chunk in range(CH):
+            part = self.at_chunk(chunk)
+            grad_one = self.scatter_chunk(started, self.own_b, chunk)
+            normed = self.n1[part, :]
+            self.xs[part, :] = (
+                self.gm[part, :] + norm_back(grad_one, normed, self.i1[part, :], gain_one)
+            ).astype(low)
+            for place, value in enumerate((grad_one * normed, grad_one)):
+                totals[place] = totals[place] + jnp.sum(value, axis=0, keepdims=True)
+        self.move_start(self.xs, self.gtok, False, move[3])
+        self.sums[0:1, :] = totals[0]
+        self.sums[1:2, :] = totals[1]
+        self.sums[6:8, :] = jnp.zeros((2, width), f32)
+        self.grads_three("q")
+        for kind in "duoq":
+            self.grads_done(kind)
+        self.move_wait(self.ox, self.out, move[2])
+        self.move_wait(self.xs, self.gtok, move[3])
+        self.drain()
+
+    def mask_blocks(self):
+        rows = self.rows
+        for block in range(4):
+            down = block * rows + lax.broadcasted_iota(jnp.int32, (rows, 1), 0)
+            side = block * rows + lax.broadcasted_iota(jnp.int32, (1, rows), 1)
+
+            def ids(places):
+                total = jnp.zeros_like(places)
+                for piece in range(4):
+                    first = self.st[piece]
+                    inside = (places >= first) & (places < first + PIECE)
+                    total = jnp.where(inside, piece + 1, total)
+                return total
+
+            mine, theirs = ids(down), ids(side)
+            seen = (side <= down) | ((mine == theirs) & (mine > 0))
+            self.mk[block] = jnp.where(seen, 0.0, -1e30).astype(jnp.bfloat16)
+
+
+IN_NAMES = ("st", "tok", "go", "in_q", "in_o", "in_u", "in_d", "small", "bq", "bu")
+OUT_NAMES = ("out", "gtok", "eq", "eo", "eu", "ed", "sums", "bsum")
+
+
+def fused_layer(starts_row, tok, go, in_q, in_o, in_u, in_d, small, bq, bu):
+    rows, width = tok.shape
+    heads, dim = 4, width // 16
+    hidden = in_u.shape[1] // 4
+    part = width // 8
+    n = 4 * rows
+    low, f32 = jnp.bfloat16, jnp.float32
+    scratch = dict(
+        xs=((rows, width), low),
+        gx=((rows, width), low),
+        wq=((3, 4, dim, width), low),
+        wo=((4, dim, width), low),
+        wu=((4, width, hidden), low),
+        wd=((4, hidden, width), low),
+        h1=((n, width), low),
+        h2=((n, width), low),
+        gg=((n, width), low),
+        ga=((n, width), low),
+        qh=((heads, n, dim), low),
+        kh=((heads, n, dim), low),
+        vh=((heads, n, dim), low),
+        hh=((heads, n, dim), low),
+        ho=((n, heads * dim), low),
+        gp=((n, 3 * heads * dim), low),
+        ka=((n, dim), f32),
+        va=((n, dim), f32),
+        mk=((4, rows, rows), low),
+        n1=((rows, width), f32),
+        n2=((rows, width), f32),
+        mid=((rows, width), f32),
+        gm=((rows, width), f32),
+        i1=((rows, 1), f32),
+        i2=((rows, 1), f32),
+        own_a=((rows, width), f32),
+        own_b=((rows, width), f32),
+        hid=((n, 4 * hidden), low),
+        gu=((n, 4 * hidden), low),
+        ox=((rows, width), low),
+        rs=((2, 5, rows, width), low),
+        rx=((3, rows, width), low),
+        dq=((3, 4, dim, width), low),
+        do=((4, dim, width), low),
+        du=((4, width, hidden), low),
+        dd=((4, hidden, width), low),
+        yq=((3, 4, dim, 4 * part), low),
+        yo=((4, dim, 4 * part), low),
+        yu=((4, 4 * part, hidden), low),
+        yd=((4, hidden, 4 * part), low),
+        zq=((3, 3, dim, 4 * part), low),
+        zo=((3, dim, 4 * part), low),
+        zu=((3, 4 * part, hidden), low),
+        zd=((3, hidden, 4 * part), low),
+        fq=((3, dim, 4 * part), low),
+        fo=((dim, 4 * part), low),
+        fu=((4 * part, hidden), low),
+        fd=((hidden, 4 * part), low),
+    )
+    probs = [((heads, rows, (block + 1) * rows), low) for block in range(4)]
+    names = IN_NAMES + OUT_NAMES + tuple(scratch)
+
+    def kernel(*refs):
+        count = len(names)
+        state = Fused(names, refs[:count])
+        state.pb = refs[count : count + 4]
+        state.ssem, state.rsem, state.lsem = refs[count + 4 :]
+        state.run()
+
+    hbm = pl.BlockSpec(memory_space=pl.ANY)
+    vmem = pl.BlockSpec(memory_space=pltpu.VMEM)
+    return pl.pallas_call(
+        kernel,
+        out_shape=(
+            jax.ShapeDtypeStruct((rows, width), low),
+            jax.ShapeDtypeStruct((rows, width), low),
+            jax.ShapeDtypeStruct((4, 3, dim, part), low),
+            jax.ShapeDtypeStruct((4, dim, part), low),
+            jax.ShapeDtypeStruct((4, part, hidden), low),
+            jax.ShapeDtypeStruct((4, hidden, part), low),
+            jax.ShapeDtypeStruct((8, width), f32),
+            jax.ShapeDtypeStruct((2, width), f32),
+        ),
+        in_specs=[pl.BlockSpec(memory_space=pltpu.SMEM)] + [hbm] * 6 + [vmem] * 3,
+        out_specs=(hbm,) * 6 + (vmem,) * 2,
+        scratch_shapes=[pltpu.VMEM(*spec) for spec in scratch.values()]
+        + [pltpu.VMEM(*spec) for spec in probs]
+        + [pltpu.SemaphoreType.DMA((SEMS,))] * 3,
+        name="fused_layer",
+        compiler_params=pltpu.CompilerParams(
+            collective_id=0, has_side_effects=True, vmem_limit_bytes=VMEM_LIMIT
+        ),
+    )(starts_row, tok, go, in_q, in_o, in_u, in_d, small, bq, bu)
+
+
+SEMS = 192
+VMEM_LIMIT = 67043328
+
+
+def per_device_fused(
+    tokens_in, starts, ln1_gain, ln1_bias, w_qkv, b_qv, w_out, b_out,
+    ln2_gain, ln2_bias, w_up, b_up, w_down, b_down, grad_out,
+):
+    rows, width = tokens_in.shape
+    f32 = jnp.float32
+    dp, z = lax.axis_index("dp"), lax.axis_index("tensor")
+    member, y = dp % 4, dp // 4
+    part = width // 8
+    dim = width // 16
+    hidden = w_up.shape[1] // 4
+    bit = ln1_gain.shape[0]
+    packed = jnp.concatenate(
+        [
+            ln1_gain, ln1_bias, b_out, ln2_gain, ln2_bias, b_down,
+            b_qv.astype(f32).reshape(-1), b_up.astype(f32).reshape(-1),
+            starts.astype(f32).reshape(-1),
+        ]
+    )
+    fill = -packed.shape[0] % 128
+    packed = jnp.concatenate([packed, jnp.zeros((fill,), f32)])[None]
+    every = lax.all_gather(packed, ("dp", "tensor"), axis=0, tiled=True)
+    small = every[:, : 6 * bit].reshape(32, 6, bit).transpose(1, 0, 2).reshape(6, width)
+    small = jnp.concatenate([small, jnp.zeros((2, width), f32)])
+    at = 6 * bit
+    qv = every[:, at : at + b_qv.size].reshape(8, 4, *b_qv.shape)
+    at += b_qv.size
+    ups = every[:, at : at + b_up.size].reshape(8, 4, *b_up.shape)
+    at += b_up.size
+    first = every[:, at : at + 4].reshape(8, 4, 4)[:, 0]
+    starts_row = lax.dynamic_index_in_dim(first, 2 * z + y, 0, keepdims=False).astype(jnp.int32)
+    qv = qv.transpose(1, 2, 0, 3).reshape(4, 4, b_qv.shape[0] // 4, 8 * b_qv.shape[1])
+    qv = lax.dynamic_index_in_dim(qv, member, 1, keepdims=False).reshape(4, 2, dim)
+    bq = jnp.stack([qv[:, 0], jnp.zeros_like(qv[:, 0]), qv[:, 1]]).reshape(1, 3 * 4 * dim)
+    ups = ups.transpose(1, 2, 0, 3).reshape(4, 4, b_up.shape[0] // 4, 8 * b_up.shape[1])
+    bu = lax.dynamic_index_in_dim(ups, member, 1, keepdims=False).reshape(1, 4 * hidden)
+    in_q = w_qkv.reshape(part, 4, 3, dim).transpose(1, 2, 3, 0)
+    in_o = w_out.reshape(4, dim, part)
+    in_d = w_down.reshape(4, hidden, part)
+    out, gtok, eq, eo, eu, ed, sums, bsum = fused_layer(
+        starts_row, tokens_in, grad_out, in_q, in_o, w_up, in_d, small, bq, bu
+    )
+    grad_w_qkv = eq.transpose(3, 0, 1, 2).reshape(part, 3 * 4 * dim).astype(f32)
+    grad_w_out = eo.reshape(4 * dim, part).astype(f32)
+    grad_w_up = eu.transpose(1, 0, 2).reshape(part, 4 * hidden).astype(f32)
+    grad_w_down = ed.reshape(4 * hidden, part).astype(f32)
+    up_sum = bsum[0, : 4 * hidden].reshape(4, 1, hidden)
+    qv_sum = bsum[1, : 3 * 4 * dim].reshape(3, 4, dim)
+    qv_sum = jnp.stack([qv_sum[0], qv_sum[2]], axis=1).reshape(4, 1, 2 * dim)
+    spot = (jnp.arange(4) == member)[None, :, None]
+    up_sum = jnp.where(spot, up_sum, 0.0)
+    qv_sum = jnp.where(spot, qv_sum, 0.0)
+    up_sum = up_sum.reshape(4, 4, b_up.shape[0] // 4, 8, b_up.shape[1]).transpose(3, 0, 1, 2, 4)
+    qv_sum = qv_sum.reshape(4, 4, b_qv.shape[0] // 4, 8, b_qv.shape[1]).transpose(3, 0, 1, 2, 4)
+    vectors = sums[:6].reshape(6, 32, bit).transpose(1, 0, 2).reshape(32, 6 * bit)
+    joined = jnp.concatenate(
+        [vectors, qv_sum.reshape(32, b_qv.size), up_sum.reshape(32, b_up.size)], axis=1
+    )
+    mine = lax.psum_scatter(joined, ("dp", "tensor"), scatter_dimension=0, tiled=True)[0]
+    take = [mine[k * bit : (k + 1) * bit] for k in range(6)]
+    at = 6 * bit
+    grad_b_qv = mine[at : at + b_qv.size].reshape(b_qv.shape)
+    grad_b_up = mine[at + b_qv.size :].reshape(b_up.shape)
+    return (
+        out, gtok, take[0], take[1], grad_w_qkv, grad_b_qv, grad_w_out, take[2],
+        take[3], take[4], grad_w_up, grad_b_up, grad_w_down, take[5],
+    )
+
+
 def solution(mesh):
+    sizes = (mesh.shape["dp"], mesh.shape["tensor"])
+
+    def layer(tokens_in, starts, *others):
+        fits = sizes == (8, 4) and tokens_in.shape[0] == PIECE and starts.shape == (1, 4)
+        return (per_device_fused if fits else per_device)(tokens_in, starts, *others)
+
     return jax.shard_map(
-        per_device,
+        layer,
         mesh=mesh,
         in_specs=(
             P(("dp", "tensor"), None),

time: 712 us -> 423 us (0.59)
  waiting for transfers between devices: 361 us -> 0 us
  Pallas kernels: 0 us -> 281 us
  matrix products: 91.2 us -> 0 us
  other arithmetic: 39.5 us -> 2.44 us
  local copies, waits for them, and re-layouts: 52.4 us -> 21.1 us
  blocking collectives: 135 us -> 115 us
  between operations: 15.3 us -> 1.05 us
  loops' own time: 8.35 us -> 0 us
    pallas_call x0 -> x1, Pallas kernels: none -> 281 us  [fused_layer(): pl.pallas_call(kernel, out_shape=(jax.ShapeDtypeStruct((rows, width), low...]
    all_gather x7 -> x0, waiting for transfers between devices: 182 us -> none  [the longest x2 72.6 us: gather_rows(): return lax.all_gather(values, 'tensor', axis=0, tiled=True)]
    reduce_scatter x6 -> x0, waiting for transfers between devices: 169 us -> none  [the longest x2 86.8 us: reduce_grads(): lax.psum_scatter(term(jnp.int32(0), lax.axis_size('tensor') * rows).astyp...]
    dot_general x26 -> x0, matrix products: 91.2 us -> none  [the longest x4 21.5 us: dot_last(): lax.dot_general(left, right, (((1,), (1,)), ((), ())), preferred_element_...]
    unnamed x3 -> x1, blocking collectives: 105 us -> 50.3 us
    all_gather x3 -> x1, blocking collectives: 30.6 us -> 64.9 us  [per_device_fused(): every = lax.all_gather(packed, ('dp', 'tensor'), axis=0, tiled=True)]
    dynamic_update_slice x4 -> x0, local copies, waits for them, and re-layouts: 22.2 us -> none  [attention_backward(): lax.scan(step, (empty, empty), (jnp.arange(total_blocks, dtype=jnp.int32)...]
    convert_element_type x14 -> x5, other arithmetic: 19.8 us -> 2.26 us  [the longest x1 0.84 us: per_device_fused(): grad_w_down = ed.reshape(4 * hidden, part).astype(f32)]
  transfers between devices with their start and end apart: 15 -> 0, of which waited for: 11 -> 0; matrix products, arithmetic and copies ran while one was open for 19% -> 0% of each run, Pallas kernels for 0% -> 0%
where the time goes in v1:
time: 423 us; the launch traced here: 421 us
  Pallas kernels  281 us (66%)
  blocking collectives  115 us (27%)
  local copies, waits for them, and re-layouts  21.1 us (5%)
    pallas_call x1, Pallas kernels, fused_layer(): pl.pallas_call(kernel, out_shape=(jax.ShapeDtypeStruct((rows, width), low...  281 us
    all_gather x1, blocking collectives, per_device_fused(): every = lax.all_gather(packed, ('dp', 'tensor'), axis=0, tiled=True)  64.9 us
    unnamed x1, blocking collectives  50.3 us
    unnamed x49, local copies, waits for them, and re-layouts  11.9 us

profile of v1, /device:TPU:1, one launch (start us, length us, event | category | flops | bytes accessed | tf_op | source)
XLA Modules:
  0.0 421.0 jit_solution(3254520711198955471)
XLA Ops:
  0.7 0.6 copy-done.19
  1.4 0.1 pad.7.clone
  1.5 0.6 broadcast_in_dim.71
  2.2 0.7 broadcast_in_dim.79
  2.9 0.1 copy.86
  3.0 0.1 reshape.167
  3.1 0.5 copy-done.11
  3.6 0.1 copy.87
  3.7 0.1 reshape.169
  3.9 0.4 copy-done.15
  4.4 0.1 copy-done.12
  4.6 0.1 concatenate.9
  4.7 64.9 %all-gather.1 = f32[32,1,512]{2,1,0:T(1,128)S(1)} all-gather(f32[1,1,512]{2,1,0:T(1,128)S(1)} %bitcast.93), channel_id=2, replica_groups=mesh['dp'=8,'tensor'=4] {'dp','tensor'}, dimensions={0}, use_global_device_ids=true | all-gather | bytes 67584 | tf_op jit(solution)/shard_map/all_gather | solution.py:1133
  69.7 0.1 copy.91
  69.8 0.1 copy.112
  69.9 0.7 convert_reduce_fusion.refs_0_
  70.6 0.1 copy.95
  70.7 0.1 reshape.153
  70.8 0.1 reshape.154
  70.9 0.6 concatenate.10.refs_7_
  71.5 0.2 copy-done.4
  71.7 0.8 copy.89
  72.5 0.1 reshape.155
  72.6 0.2 copy.92
  72.8 0.1 reshape.156
  73.1 0.1 reshape.157
  73.2 0.7 reshape.158.refs_8_
  73.9 0.2 reshape.159
  74.1 0.3 copy.96
  74.4 0.1 reshape.160
  74.6 0.7 reshape.161.refs_9_
  75.3 281.2 %fused_layer.1 = (bf16[256,1024]{1,0:T(8,128)(2,1)}, bf16[256,1024]{1,0:T(8,128)(2,1)}, bf16[4,3,64,128]{3,2,1,0:T(8,128)(2,1)}, bf16[4,64,128]{2,1,0:T(8,128)(2...) custom-call(s32[4]{0:T(128)} %convert_reduce_fusion.refs_0_, ...), custom_call_target="tpu_custom_call" | custom-call | tf_op jit(solution)/shard_map/fused_layer/pallas_call | solution.py:1084
  356.5 0.7 copy-done.8
  357.2 0.1 stack_squeeze.14
  357.3 0.1 stack_squeeze.15
  357.4 0.1 copy.99
  357.5 0.7 copy-done.7
  358.3 0.1 reshape.162
  358.5 0.1 reshape.163
  358.5 0.7 copy-done.6
  359.3 0.7 bitcast_convert_fusion.1
  360.0 0.1 broadcast_in_dim.76
  360.2 0.6 copy-done.10
  360.8 0.2 broadcast_in_dim.81
  361.0 0.9 copy.102
  361.9 0.2 broadcast_in_dim.84
  362.2 0.6 copy-done.9
  362.8 0.1 pad_maximum_fusion
  362.8 50.3 %all-reduce.1 = f32[32,384]{1,0:T(8,128)S(1)} all-reduce(f32[32,384]{1,0:T(8,128)S(1)} %pad_maximum_fusion), channel_id=3, replica_groups=mesh['dp'=8,'tensor'=4] {'dp','tensor'}, use_global_device_ids=true, to_apply=%region_0.1.clone | all-reduce | flops 12288 | bytes 98304
  413.2 0.1 dynamic-slice_reduce_fusion
  413.3 0.1 dynamic-slice_reduce_fusion.1
  413.4 0.6 dynamic-slice_bitcast_fusion
  414.0 0.1 reshape.164
  414.1 0.6 copy.106
  414.7 0.1 reshape.165
  414.8 0.6 copy.108
  415.5 0.9 copy.105
  416.5 0.2 copy.104
  416.7 1.0 copy.107
  417.7 0.8 bitcast_convert_fusion
  418.6 0.4 copy-done.1
  419.0 0.8 copy.120
  419.8 0.4 copy-done
  420.2 0.8 copy.121
  (60 shorter events, 1.1 us)
Async XLA Ops:
  0.7 0.7 copy-start.19
  2.2 0.7 copy-start.18
  3.0 0.7 copy-start.11
  3.7 0.7 copy-start.15
  3.7 0.7 copy-start.16
  3.7 0.7 copy-start.17
  3.9 0.7 copy-start.12
  3.9 0.7 copy-start.13
  3.9 0.7 copy-start.14
  70.7 0.9 copy-start.4
  356.5 0.7 copy-start.8
  357.5 0.8 copy-start.7
  358.4 0.8 copy-start.6
  360.1 0.7 copy-start.10
  362.1 0.7 copy-start.9
  362.8 52.7 %copy-start.5 = (bf16[4,3,64,128]{3,2,1,0:T(8,128)(2,1)S(1)}, bf16[4,3,64,128]{3,2,1,0:T(8,128)(2,1)}, u32[]{:S(2)}) copy-start(bf16[4,3,64,128]{3,2,1,0:T(8,128)(2,1)} %get-tuple-element.26) | copy-start | bytes 589828
  415.5 1.0 copy-start.3
  416.7 1.0 copy-start.2
  417.7 1.2 copy-start.1
  419.0 1.2 copy-start

commit v2 on v1

--- a/solution.py
+++ b/solution.py
@@ -352,15 +352,16 @@
         self.next_sem = 0
         self.unsent = []
         self.groups = {0: [], 1: []}
+        self.unsent_later = []
         dp, self.z = lax.axis_index("dp"), lax.axis_index("tensor")
         self.y, self.x, self.c = dp // 4, (dp // 2) % 2, dp % 2
-        self.j = 2 * self.x + self.c
+        self.j = self.member(self.x, self.c)
         self.q = self.quarter(self.j)
         self.sib = self.dev(self.y, self.x, 1 - self.c, self.z)
         self.across = self.dev(self.y, 1 - self.x, self.c, self.z)
-        self.q_sib = self.quarter(2 * self.x + 1 - self.c)
-        self.q_x = self.quarter(2 * (1 - self.x) + self.c)
-        self.q_d = self.quarter(2 * (1 - self.x) + 1 - self.c)
+        self.q_sib = self.quarter(self.member(self.x, 1 - self.c))
+        self.q_x = self.quarter(self.member(1 - self.x, self.c))
+        self.q_d = self.quarter(self.member(1 - self.x, 1 - self.c))
         self.rows = self.tok.shape[0]
         self.width = self.tok.shape[1]
         self.part = self.width // 8
@@ -368,19 +369,28 @@
     def dev(self, y, x, c, z):
         return ((y * 2 + x) * 2 + c, z)
 
+    def member(self, x, c):
+        return 2 * c + x
+
+    def local(self, member):
+        return 2 * (member % 2) + member // 2
+
+    def mate(self, member):
+        return self.dev(self.y, member % 2, member // 2, self.z)
+
     def quarter(self, member):
         return (member - self.z + 4) % 4
 
-    def sem(self):
+    def sem(self, count=1):
         index = self.next_sem
-        self.next_sem += 1
+        self.next_sem += count
         return index
 
-    def copy(self, src, dst, device, index):
+    def copy(self, src, dst, device, index, sent=None):
         return pltpu.make_async_remote_copy(
             src_ref=src,
             dst_ref=dst,
-            send_sem=self.ssem.at[index],
+            send_sem=self.ssem.at[index if sent is None else sent],
             recv_sem=self.rsem.at[index],
             device_id=device,
             device_id_type=MESH,
@@ -391,12 +401,21 @@
         copy.start()
         (self.unsent if group is None else self.groups[group]).append(copy)
 
+    def later(self, view, sent, when=None):
+        self.unsent_later.append((view, sent, when))
+
     def arrived(self, dst, index):
         self.copy(dst, dst, self.sib, index).wait_recv()
 
     def drain(self):
         for copy in self.unsent + self.groups[0] + self.groups[1]:
             copy.wait_send()
+        for view, sent, when in self.unsent_later:
+            copy = self.copy(view(), view(), self.sib, sent)
+            if when is None:
+                copy.wait_send()
+            else:
+                pl.when(when)(copy.wait_send)
 
     def at_quarter(self, quarter, chunk=None):
         if chunk is None:
@@ -425,7 +444,7 @@
     def homes(self):
         plane = 2 * self.y + self.x
         member = (plane + self.z) % 4
-        worker = (self.c, member // 2, member % 2, plane)
+        worker = (self.c, member % 2, member // 2, plane)
         owner = (self.z // 2, self.z % 2, self.y, self.q)
         same = (
             (worker[0] == self.y)
@@ -469,8 +488,6 @@
         return pl.ds(pl.multiple_of(source * self.part, self.part), self.part)
 
     def cut(self, kind, ref, zc, where):
-        if kind == "q":
-            return ref.at[:, zc, :, where]
         if kind == "u":
             return ref.at[zc, where, :]
         return ref.at[zc, :, where]
@@ -482,19 +499,16 @@
         return ref.at[member]
 
     def weights_one(self, kind):
-        source = self.dev(self.y, self.x, self.c, self.z)[0]
+        source = 4 * self.y + self.local(self.j)
         here = self.cut(kind, self.wbuf[kind], self.z, self.place(source))
         self.one[kind] = []
         for step in range(1, 4):
             member = (self.j + step) % 4
             index = self.sem()
             self.send(
-                self.piece(kind, self.shard[kind], member),
-                here,
-                self.dev(self.y, member // 2, member % 2, self.z),
-                index,
+                self.piece(kind, self.shard[kind], member), here, self.mate(member), index
             )
-            sender = self.y * 4 + (self.j - step + 4) % 4
+            sender = 4 * self.y + self.local((self.j - step + 4) % 4)
             self.one[kind].append(
                 (self.cut(kind, self.wbuf[kind], self.z, self.place(sender)), index)
             )
@@ -504,35 +518,81 @@
         )
         local.start()
         self.own[kind] = local
+        self.two[kind] = self.sem(4)
+        self.three[kind] = self.sem(4)
+        self.pass_sem[kind] = self.sem()
+
+    def mine(self, kind, plane):
+        return self.cut(kind, self.wbuf[kind], plane, self.span(self.y))
 
     def weights_two(self, kind):
         self.own[kind].wait()
         for view, index in self.one[kind]:
             self.arrived(view, index)
-        mine = self.cut(kind, self.wbuf[kind], self.z, self.span(self.y))
-        self.two[kind] = []
-        for step in range(1, 4):
+        here = self.mine(kind, self.z)
+        for step, when in ((2, None), (1, self.z != 3), (3, self.z != 0)):
             plane = (self.z + step) % 4
-            index = self.sem()
-            self.send(mine, mine, self.dev(self.y, self.x, self.c, plane), index)
-            self.two[kind].append(((self.z - step + 4) % 4, index))
-        self.three[kind] = []
-        self.weights_cross(kind, self.z)
-
-    def weights_cross(self, kind, plane):
-        index = self.sem()
-        mine = self.cut(kind, self.wbuf[kind], plane, self.span(self.y))
-        self.send(mine, mine, self.dev(1 - self.y, self.x, self.c, self.z), index)
-        self.three[kind].append((plane, index))
-
-    def weights_three(self, kind):
-        for plane, index in self.two[kind]:
-            self.arrived(self.cut(kind, self.wbuf[kind], plane, self.span(self.y)), index)
-            self.weights_cross(kind, plane)
+            index = self.two[kind] + step
+            copy = self.copy(here, here, self.dev(self.y, self.x, self.c, plane), index)
+            if when is None:
+                copy.start()
+            else:
+                pl.when(when)(copy.start)
+            self.later(lambda: self.mine(kind, self.z), index, when)
+
+    def weights_relay(self, kind, guard=None):
+        for here, plane, step in ((2, 3, 3), (1, 0, 1)):
+            when = self.z == here
+            block = self.mine(kind, (here + 2) % 4)
+            copy = self.copy(
+                block,
+                block,
+                self.dev(self.y, self.x, self.c, plane),
+                self.two[kind] + step,
+                self.pass_sem[kind],
+            )
+            pl.when(when if guard is None else when & guard)(copy.start)
+
+    def relayed(self, kind):
+        self.later(
+            lambda: self.mine(kind, self.z), self.pass_sem[kind], (self.z == 1) | (self.z == 2)
+        )
+        for step in range(4):
+            self.later(lambda: self.mine(kind, self.z), self.three[kind] + step)
+
+    def weights_cross(self, kind, step):
+        mine = self.mine(kind, (self.z - step + 4) % 4)
+        self.copy(
+            mine,
+            mine,
+            self.dev(1 - self.y, self.x, self.c, self.z),
+            self.three[kind] + step,
+        ).start()
+
+    def weights_here(self, kind, step):
+        self.arrived(self.mine(kind, (self.z - step + 4) % 4), self.two[kind] + step)
+
+    def weights_three(self, kind, steps=(1, 3)):
+        for step in steps:
+            self.weights_here(kind, step)
+            self.weights_cross(kind, step)
+
+    def weights_start_three(self, kind):
+        self.weights_cross(kind, 0)
+        self.weights_here(kind, 2)
+        self.weights_relay(kind)
+        self.weights_cross(kind, 2)
+
+    def weights_ready(self, kind, step):
+        plane = (self.z - step + 4) % 4
+        self.arrived(
+            self.cut(kind, self.wbuf[kind], plane, self.span(1 - self.y)),
+            self.three[kind] + step,
+        )
 
     def weights_done(self, kind):
-        for plane, index in self.three[kind]:
-            self.arrived(self.cut(kind, self.wbuf[kind], plane, self.span(1 - self.y)), index)
+        for step in range(4):
+            self.weights_ready(kind, step)
 
     def grads_one(self, kind):
         index = self.sem()
@@ -564,6 +624,30 @@
             )
             self.swaps[kind].append(index)
 
+    def head_one(self, step, head):
+        self.copy(
+            self.cut("q", self.dq, head, self.span(1 - self.y)),
+            self.cut("q", self.yq, head, slice(None)),
+            self.dev(1 - self.y, self.x, self.c, self.z),
+            self.head_y + step,
+        ).start()
+
+    def head_add(self, step, head):
+        there = self.cut("q", self.yq, head, slice(None))
+        self.arrived(there, self.head_y + step)
+        mine = self.cut("q", self.dq, head, self.span(self.y))
+        mine[...] = (mine[...].astype(jnp.float32) + there[...].astype(jnp.float32)).astype(
+            jnp.bfloat16
+        )
+
+    def head_two(self, step, head):
+        self.copy(
+            self.cut("q", self.dq, head, self.span(self.y)),
+            self.zq.at[step],
+            self.dev(self.y, self.x, self.c, head),
+            self.head_z + step,
+        ).start()
+
     def grads_three(self, kind):
         mine = self.cut(kind, self.dbuf[kind], self.z, self.span(self.y))
         total = mine[...].astype(jnp.float32)
@@ -579,23 +663,21 @@
             member = (self.j + step) % 4
             index = self.sem()
             self.send(
-                self.slab(kind, final, member),
+                self.slab(kind, final, self.local(member)),
                 ends.at[self.j],
-                self.dev(self.y, member // 2, member % 2, self.z),
+                self.mate(member),
                 index,
             )
             self.last[kind].append(((self.j - step + 4) % 4, index))
         index = self.sem()
         local = pltpu.make_async_copy(
-            self.slab(kind, final, self.j), ends.at[self.j], self.lsem.at[index]
+            self.slab(kind, final, self.local(self.j)), ends.at[self.j], self.lsem.at[index]
         )
         local.start()
         self.own[kind] = local
 
     def slab(self, kind, ref, member):
         where = pl.ds(pl.multiple_of(member * self.part, self.part), self.part)
-        if kind == "q":
-            return ref.at[:, :, where]
         if kind == "u":
             return ref.at[where, :]
         return ref.at[:, where]
@@ -604,6 +686,95 @@
         self.own[kind].wait()
         for member, index in self.last[kind]:
             self.arrived(self.ebuf[kind].at[member], index)
+
+    def small_one(self):
+        self.sma[self.z] = self.si[...]
+        self.small_sem = [self.sem() for _ in range(3)]
+        for step in range(1, 4):
+            plane = (self.z + step) % 4
+            self.send(
+                self.si,
+                self.sma.at[self.z],
+                self.dev(self.y, self.x, self.c, plane),
+                self.small_sem[step - 1],
+            )
+
+    def around(self, step):
+        return (lax.axis_index("dp") + step + 8) % 8
+
+    def small_two(self):
+        for step in range(1, 4):
+            self.arrived(self.sma.at[(self.z - step + 4) % 4], self.small_sem[step - 1])
+        me = self.around(0)
+        self.lb[me] = sum(self.sma[plane, 0] for plane in range(4))
+        self.bb[me] = self.sma[:, 1 + self.j]
+        self.plane_sem = [(self.sem(), self.sem()) for _ in range(7)]
+        for step in range(1, 8):
+            other = self.around(step)
+            member = self.member((other // 2) % 2, other % 2)
+            first, second = self.plane_sem[step - 1]
+            self.send(self.lb.at[me], self.lb.at[me], (other, self.z), first)
+            self.send(self.sma.at[:, 1 + member], self.bb.at[me], (other, self.z), second)
+
+    def small_three(self):
+        for step in range(1, 8):
+            other = self.around(-step)
+            first, second = self.plane_sem[step - 1]
+            self.arrived(self.lb.at[other], first)
+            self.arrived(self.bb.at[other], second)
+        part, dim = self.part, self.qh.shape[2]
+        for source in range(8):
+            self.small[:, source * part : (source + 1) * part] = self.lb[source]
+        bias = sum(self.bb[source] for source in range(8))
+        for head in range(4):
+            row = bias[head, 0:1]
+            self.bq[head, :, 0:dim] = row[:, 0:dim]
+            self.bq[head, :, dim : 2 * dim] = jnp.zeros((1, dim), jnp.float32)
+            self.bq[head, :, 2 * dim :] = row[:, dim:]
+            for half in range(2):
+                place = (2 * head + half) * part
+                self.bu[:, place : place + part] = bias[head, 1 + half : 2 + half]
+
+    def back_one(self):
+        part, me = self.part, self.around(0)
+        for target in range(8):
+            self.cs[target] = self.sums[:, target * part : (target + 1) * part]
+        self.cr[me] = self.cs[me]
+        self.cd[me] = self.cb[...]
+        self.back_sem = [(self.sem(), self.sem()) for _ in range(7)]
+        for step in range(1, 8):
+            other = self.around(step)
+            first, second = self.back_sem[step - 1]
+            self.send(self.cs.at[other], self.cr.at[me], (other, self.z), first)
+            self.send(self.cb, self.cd.at[me], (other, self.z), second)
+
+    def back_two(self):
+        for step in range(1, 8):
+            other = self.around(-step)
+            first, second = self.back_sem[step - 1]
+            self.arrived(self.cr.at[other], first)
+            self.arrived(self.cd.at[other], second)
+        self.es[self.z] = sum(self.cr[source] for source in range(8))
+        for member in range(4):
+            pair = [2 * (member % 2) + member // 2, 4 + 2 * (member % 2) + member // 2]
+            self.ed_small[:, member] = self.cd[pair[0]] + self.cd[pair[1]]
+        self.eb[self.z] = self.ed_small[self.z]
+        self.line_sem = [(self.sem(), self.sem()) for _ in range(3)]
+        for step in range(1, 4):
+            plane = (self.z + step) % 4
+            device = self.dev(self.y, self.x, self.c, plane)
+            first, second = self.line_sem[step - 1]
+            self.send(self.es.at[self.z], self.es.at[self.z], device, first)
+            self.send(self.ed_small.at[plane], self.eb.at[self.z], device, second)
+
+    def back_three(self):
+        for step in range(1, 4):
+            plane = (self.z - step + 4) % 4
+            first, second = self.line_sem[step - 1]
+            self.arrived(self.es.at[plane], first)
+            self.arrived(self.eb.at[plane], second)
+        self.fs[...] = sum(self.es[plane] for plane in range(4))
+        self.fb[...] = sum(self.eb[plane] for plane in range(4))
 
     def gather_plan(self):
         return {kind: [self.sem() for _ in range(CH)] for kind in ("across", "sib", "pass")}
@@ -684,20 +855,31 @@
         self.ebuf = dict(q=self.eq, o=self.eo, u=self.eu, d=self.ed)
         self.one, self.two, self.three, self.own = {}, {}, {}, {}
         self.back, self.backs, self.swaps, self.last = {}, {}, {}, {}
-        gain_one, shift_one = self.small[0:1, :], self.small[1:2, :]
-        bias_out = self.small[2:3, :]
-        gain_two, shift_two = self.small[3:4, :], self.small[4:5, :]
-        bias_down = self.small[5:6, :]
+        self.pass_sem = {}
         heads, dim = self.qh.shape[0], self.qh.shape[2]
         hidden = self.wu.shape[2]
 
         self.barrier()
         move = [self.sem() for _ in range(4)]
+        self.small_one()
         self.move_start(self.tok, self.xs, True, move[0])
         for kind in "qoud":
             self.weights_one(kind)
         plan_one, plan_two, plan_go, plan_mid = (self.gather_plan() for _ in range(4))
         self.weights_two("q")
+        self.weights_cross("q", 0)
+        self.small_two()
+        for kind in "ou":
+            self.weights_two(kind)
+        landed = pl.ds(pl.multiple_of(self.z * rows, rows), rows)
+        own_rows = self.at_quarter(self.q)
+        self.move_start(self.go, self.gg.at[landed], True, move[1])
+        self.weights_two("d")
+        self.small_three()
+        gain_one, shift_one = self.small[0:1, :], self.small[1:2, :]
+        bias_out = self.small[2:3, :]
+        gain_two, shift_two = self.small[3:4, :], self.small[4:5, :]
+        bias_down = self.small[5:6, :]
         self.move_wait(self.tok, self.xs, move[0])
 
         for chunk in range(CH):
@@ -707,37 +889,53 @@
             self.i1[part, :] = inverse
             self.h1[self.at_quarter(self.q, chunk), :] = (normed * gain_one + shift_one).astype(low)
             self.gather_send(self.h1, plan_one, chunk)
-        for kind in "ou":
-            self.weights_two(kind)
-        self.move_start(self.go, self.gx, True, move[1])
-        self.weights_two("d")
         self.mask_blocks()
-        self.weights_three("q")
         self.gather_sib(self.h1, plan_one)
         self.gather_pass(self.h1, plan_one)
-        self.weights_done("q")
         self.gather_last(self.h1, plan_one)
 
-        def project(block, carry):
-            place = pl.ds(pl.multiple_of(block * rows, rows), rows)
-            weight = self.wq[...].reshape(3 * heads * dim, width)
-            both = dot_last(self.h1[place, :], weight) + self.bq[...]
-            for head in range(heads):
+        def parts_of(block):
+            return ([(0, block * rows)] if block else []) + [(block * rows, rows)]
+
+        near = 1 + 2 * ((3 - self.z) // 3)
+
+        def turn(step):
+            late, odd = step // 2, step % 2
+            return (1 - late) * 2 * odd + late * (near + odd * (4 - 2 * near))
+
+        def attend(step, carry):
+            back = turn(step)
+            head = (self.z - back + 4) % 4
+            self.weights_ready("q", back)
+
+            def project(block, carry):
+                place = pl.ds(pl.multiple_of(block * rows, rows), rows)
+                both = dot_last(self.h1[place, :], self.wq[head]) + self.bq[head]
                 for slot, ref in enumerate((self.qh, self.kh, self.vh)):
-                    first = (slot * heads + head) * dim
-                    value = both[:, first : first + dim].astype(low)
+                    value = both[:, slot * dim : (slot + 1) * dim].astype(low)
                     if slot == 0:
                         value = (value.astype(f32) * 0.125).astype(low)
                     ref[head, place, :] = value
-            return carry
-
-        lax.fori_loop(0, 4, project, 0)
-        self.weights_three("o")
-
-        def parts_of(block):
-            return ([(0, block * rows)] if block else []) + [(block * rows, rows)]
-
-        def attend(head, carry):
+                return carry
+
+            lax.fori_loop(0, 4, project, 0)
+
+            @pl.when(step < 3)
+            def _():
+                coming = turn(step + 1)
+                self.weights_here("q", coming)
+                self.weights_relay("q", step == 0)
+                self.weights_cross("q", coming)
+
+            @pl.when(step == 2)
+            def _():
+                self.weights_start_three("o")
+                self.weights_three("o")
+
+            @pl.when(step == 3)
+            def _():
+                self.weights_start_three("u")
+
             for block in quarters:
                 place = pl.ds(block * rows, rows)
                 query = self.qh[head, place, :]
@@ -766,6 +964,8 @@
             return carry
 
         lax.fori_loop(0, heads, attend, 0)
+        for kind in "qou":
+            self.relayed(kind)
 
         def assemble(target, refs, count):
             def one(block, carry):
@@ -778,7 +978,6 @@
 
         assemble(self.ho, (self.hh,), heads)
         self.weights_done("o")
-        self.weights_three("u")
 
         flat_out = lambda: self.wo[...].reshape(heads * dim, width)
         started = self.scatter_start(
@@ -789,6 +988,7 @@
             0,
             self.rx.at[0],
         )
+        self.weights_three("u")
         for chunk in range(CH):
             part = self.at_chunk(chunk)
             summed = self.scatter_chunk(started, self.own_a, chunk)
@@ -799,8 +999,12 @@
             self.i2[part, :] = inverse
             self.h2[self.at_quarter(self.q, chunk), :] = (normed * gain_two + shift_two).astype(low)
             self.gather_send(self.h2, plan_two, chunk)
-        self.weights_three("d")
+        self.move_wait(self.go, self.gg.at[landed], move[1])
+        for chunk in range(CH):
+            self.gather_send(self.gg, plan_go, chunk)
         self.weights_done("u")
+        self.weights_start_three("d")
+        self.relayed("d")
 
         def up(quarter):
             place = self.at_quarter(quarter)
@@ -821,11 +1025,7 @@
 
         self.gathered(self.h2, plan_two, up)
 
-        self.move_wait(self.go, self.gx, move[1])
-        for chunk in range(CH):
-            part = self.at_chunk(chunk)
-            self.gg[self.at_quarter(self.q, chunk), :] = self.gx[part, :]
-            self.gather_send(self.gg, plan_go, chunk)
+        self.weights_three("d")
         self.weights_done("d")
         flat_down = lambda: self.wd[...].reshape(4 * hidden, width)
         started_down = self.scatter_start(
@@ -843,7 +1043,7 @@
             self.gu[place, :] = (self.gu[place, :].astype(f32) * value).astype(low)
 
         self.gathered(self.gg, plan_go, to_up)
-        grad_out = self.gx[...].astype(f32)
+        grad_out = self.gg[own_rows, :].astype(f32)
         self.sums[5:6, :] = jnp.sum(grad_out, axis=0, keepdims=True)
 
         def two_part(quarter):
@@ -878,7 +1078,7 @@
             part = self.at_chunk(chunk)
             grad_two = self.scatter_chunk(started, self.own_a, chunk)
             normed = self.n2[part, :]
-            middle = self.gx[part, :].astype(f32) + norm_back(
+            middle = self.gg[self.at_quarter(self.q, chunk), :].astype(f32) + norm_back(
                 grad_two, normed, self.i2[part, :], gain_two
             )
             self.gm[part, :] = middle
@@ -889,7 +1089,12 @@
         self.sums[3:4, :] = totals[0]
         self.sums[4:5, :] = totals[1]
         self.sums[2:3, :] = totals[2]
-        self.bsum[0:1, :] = jnp.sum(self.gu[...].astype(f32), axis=0, keepdims=True)
+        up_sum = jnp.sum(self.gu[...].astype(f32), axis=0, keepdims=True)
+        lanes = self.part
+        for place in range(8):
+            self.cb[place // 2, 1 + place % 2 : 2 + place % 2, :] = up_sum[
+                :, place * lanes : (place + 1) * lanes
+            ]
         for chunk in range(CH):
             part = self.at_chunk(chunk)
             summed = self.scatter_chunk(started_down, self.own_b, chunk)
@@ -908,7 +1113,10 @@
         self.do[...] = dot_first(self.ho[...], self.ga[...]).astype(low).reshape(self.do.shape)
         self.grads_one("o")
 
-        def attend_back(head, carry):
+        self.head_y, self.head_z = self.sem(4), self.sem(3)
+
+        def attend_back(step, carry):
+            head = (self.z + 1 + step) % 4
             self.ka[...] = jnp.zeros_like(self.ka)
             self.va[...] = jnp.zeros_like(self.va)
             for block in quarters:
@@ -935,38 +1143,48 @@
                     )
                     self.ka[span, :] += dot_first(score, query)
                 self.qh[head, place, :] = (result * 0.125).astype(low)
-            self.kh[head] = self.ka[...].astype(low)
-            self.vh[head] = self.va[...].astype(low)
+            self.gp[head, :, 0:dim] = self.qh[head]
+            self.gp[head, :, dim : 2 * dim] = self.ka[...].astype(low)
+            self.gp[head, :, 2 * dim :] = self.va[...].astype(low)
+            self.dq[head] = dot_first(self.gp[head], self.h1[...]).astype(low)
+            self.head_one(step, head)
+
+            @pl.when(step > 0)
+            def _():
+                before = (self.z + step) % 4
+                self.head_add(step - 1, before)
+                self.head_two(step - 1, before)
+
             return carry
 
         lax.fori_loop(0, heads, attend_back, 0)
-        assemble(self.gp, (self.qh, self.kh, self.vh), heads)
+        self.swaps["q"] = [self.head_z + step for step in range(3)]
+        for step in range(4):
+            self.later(lambda: self.cut("q", self.dq, 0, self.span(0)), self.head_y + step)
+        for step in range(3):
+            self.later(lambda: self.zq.at[0], self.head_z + step)
         self.grads_three("d")
         self.grads_three("u")
-
-        def project_grad(slot, carry):
-            lanes = pl.ds(pl.multiple_of(slot * heads * dim, heads * dim), heads * dim)
-            value = dot_first(self.gp[:, lanes], self.h1[...]).astype(low)
-            self.dq[slot] = value.reshape(heads, dim, width)
-            return carry
-
-        lax.fori_loop(0, 3, project_grad, 0)
-        self.grads_one("q")
         self.grads_two("o")
         started = self.scatter_start(
-            lambda quarter: jnp.dot(
-                self.gp[self.at_quarter(quarter), :],
-                self.wq[...].reshape(3 * heads * dim, width),
-                preferred_element_type=f32,
+            lambda quarter: sum(
+                jnp.dot(
+                    self.gp[head, self.at_quarter(quarter), :],
+                    self.wq[head],
+                    preferred_element_type=f32,
+                )
+                for head in range(heads)
             ),
             self.own_b,
             1,
             self.rx.at[2],
         )
-        self.bsum[1:2, : 3 * heads * dim] = jnp.sum(
-            self.gp[...].astype(f32), axis=0, keepdims=True
-        )
-        self.grads_two("q")
+        for head in range(heads):
+            total = jnp.sum(self.gp[head].astype(f32), axis=0, keepdims=True)
+            self.cb[head, 0:1, 0:dim] = total[:, 0:dim]
+            self.cb[head, 0:1, dim:] = total[:, 2 * dim :]
+            self.cb[head, 3:, :] = jnp.zeros((5, self.part), f32)
+        self.head_add(3, self.z)
         self.grads_three("o")
         totals = [0.0] * 2
         for chunk in range(CH):
@@ -978,19 +1196,23 @@
             ).astype(low)
             for place, value in enumerate((grad_one * normed, grad_one)):
                 totals[place] = totals[place] + jnp.sum(value, axis=0, keepdims=True)
-        self.move_start(self.xs, self.gtok, False, move[3])
         self.sums[0:1, :] = totals[0]
         self.sums[1:2, :] = totals[1]
         self.sums[6:8, :] = jnp.zeros((2, width), f32)
+        self.back_one()
+        self.move_start(self.xs, self.gtok, False, move[3])
         self.grads_three("q")
+        self.back_two()
         for kind in "duoq":
             self.grads_done(kind)
         self.move_wait(self.ox, self.out, move[2])
+        self.back_three()
         self.move_wait(self.xs, self.gtok, move[3])
         self.drain()
 
     def mask_blocks(self):
         rows = self.rows
+        begins = self.lb[2 * self.z + self.y, 6:7, 0:4].astype(jnp.int32)
         for block in range(4):
             down = block * rows + lax.broadcasted_iota(jnp.int32, (rows, 1), 0)
             side = block * rows + lax.broadcasted_iota(jnp.int32, (1, rows), 1)
@@ -998,7 +1220,7 @@
             def ids(places):
                 total = jnp.zeros_like(places)
                 for piece in range(4):
-                    first = self.st[piece]
+                    first = begins[:, piece : piece + 1]
                     inside = (places >= first) & (places < first + PIECE)
                     total = jnp.where(inside, piece + 1, total)
                 return total
@@ -1008,11 +1230,11 @@
             self.mk[block] = jnp.where(seen, 0.0, -1e30).astype(jnp.bfloat16)
 
 
-IN_NAMES = ("st", "tok", "go", "in_q", "in_o", "in_u", "in_d", "small", "bq", "bu")
-OUT_NAMES = ("out", "gtok", "eq", "eo", "eu", "ed", "sums", "bsum")
-
-
-def fused_layer(starts_row, tok, go, in_q, in_o, in_u, in_d, small, bq, bu):
+IN_NAMES = ("tok", "go", "in_q", "in_o", "in_u", "in_d", "si")
+OUT_NAMES = ("out", "gtok", "eq", "eo", "eu", "ed", "fs", "fb")
+
+
+def fused_layer(tok, go, in_q, in_o, in_u, in_d, si):
     rows, width = tok.shape
     heads, dim = 4, width // 16
     hidden = in_u.shape[1] // 4
@@ -1021,8 +1243,7 @@
     low, f32 = jnp.bfloat16, jnp.float32
     scratch = dict(
         xs=((rows, width), low),
-        gx=((rows, width), low),
-        wq=((3, 4, dim, width), low),
+        wq=((4, 3 * dim, width), low),
         wo=((4, dim, width), low),
         wu=((4, width, hidden), low),
         wd=((4, hidden, width), low),
@@ -1035,7 +1256,7 @@
         vh=((heads, n, dim), low),
         hh=((heads, n, dim), low),
         ho=((n, heads * dim), low),
-        gp=((n, 3 * heads * dim), low),
+        gp=((heads, n, 3 * dim), low),
         ka=((n, dim), f32),
         va=((n, dim), f32),
         mk=((4, rows, rows), low),
@@ -1052,22 +1273,36 @@
         ox=((rows, width), low),
         rs=((2, 5, rows, width), low),
         rx=((3, rows, width), low),
-        dq=((3, 4, dim, width), low),
+        dq=((4, 3 * dim, width), low),
         do=((4, dim, width), low),
         du=((4, width, hidden), low),
         dd=((4, hidden, width), low),
-        yq=((3, 4, dim, 4 * part), low),
+        yq=((4, 3 * dim, 4 * part), low),
         yo=((4, dim, 4 * part), low),
         yu=((4, 4 * part, hidden), low),
         yd=((4, hidden, 4 * part), low),
-        zq=((3, 3, dim, 4 * part), low),
+        zq=((3, 3 * dim, 4 * part), low),
         zo=((3, dim, 4 * part), low),
         zu=((3, 4 * part, hidden), low),
         zd=((3, hidden, 4 * part), low),
-        fq=((3, dim, 4 * part), low),
+        fq=((3 * dim, 4 * part), low),
         fo=((dim, 4 * part), low),
         fu=((4 * part, hidden), low),
         fd=((hidden, 4 * part), low),
+        small=((8, width), f32),
+        sums=((8, width), f32),
+        bq=((4, 1, 3 * dim), f32),
+        bu=((1, 4 * hidden), f32),
+        sma=((4, 5, 8, part), f32),
+        lb=((8, 8, part), f32),
+        bb=((8, 4, 8, part), f32),
+        cs=((8, 8, part), f32),
+        cr=((8, 8, part), f32),
+        cb=((4, 8, part), f32),
+        cd=((8, 4, 8, part), f32),
+        es=((4, 8, part), f32),
+        ed_small=((4, 4, 8, part), f32),
+        eb=((4, 4, 8, part), f32),
     )
     probs = [((heads, rows, (block + 1) * rows), low) for block in range(4)]
     names = IN_NAMES + OUT_NAMES + tuple(scratch)
@@ -1086,14 +1321,14 @@
         out_shape=(
             jax.ShapeDtypeStruct((rows, width), low),
             jax.ShapeDtypeStruct((rows, width), low),
-            jax.ShapeDtypeStruct((4, 3, dim, part), low),
+            jax.ShapeDtypeStruct((4, 3 * dim, part), low),
             jax.ShapeDtypeStruct((4, dim, part), low),
             jax.ShapeDtypeStruct((4, part, hidden), low),
             jax.ShapeDtypeStruct((4, hidden, part), low),
-            jax.ShapeDtypeStruct((8, width), f32),
-            jax.ShapeDtypeStruct((2, width), f32),
+            jax.ShapeDtypeStruct((8, part), f32),
+            jax.ShapeDtypeStruct((4, 8, part), f32),
         ),
-        in_specs=[pl.BlockSpec(memory_space=pltpu.SMEM)] + [hbm] * 6 + [vmem] * 3,
+        in_specs=[hbm] * 6 + [vmem],
         out_specs=(hbm,) * 6 + (vmem,) * 2,
         scratch_shapes=[pltpu.VMEM(*spec) for spec in scratch.values()]
         + [pltpu.VMEM(*spec) for spec in probs]
@@ -1102,10 +1337,10 @@
         compiler_params=pltpu.CompilerParams(
             collective_id=0, has_side_effects=True, vmem_limit_bytes=VMEM_LIMIT
         ),
-    )(starts_row, tok, go, in_q, in_o, in_u, in_d, small, bq, bu)
-
-
-SEMS = 192
+    )(tok, go, in_q, in_o, in_u, in_d, si)
+
+
+SEMS = 256
 VMEM_LIMIT = 67043328
 
 
@@ -1116,62 +1351,43 @@
     rows, width = tokens_in.shape
     f32 = jnp.float32
     dp, z = lax.axis_index("dp"), lax.axis_index("tensor")
-    member, y = dp % 4, dp // 4
     part = width // 8
     dim = width // 16
     hidden = w_up.shape[1] // 4
     bit = ln1_gain.shape[0]
-    packed = jnp.concatenate(
-        [
-            ln1_gain, ln1_bias, b_out, ln2_gain, ln2_bias, b_down,
-            b_qv.astype(f32).reshape(-1), b_up.astype(f32).reshape(-1),
-            starts.astype(f32).reshape(-1),
-        ]
-    )
-    fill = -packed.shape[0] % 128
-    packed = jnp.concatenate([packed, jnp.zeros((fill,), f32)])[None]
-    every = lax.all_gather(packed, ("dp", "tensor"), axis=0, tiled=True)
-    small = every[:, : 6 * bit].reshape(32, 6, bit).transpose(1, 0, 2).reshape(6, width)
-    small = jnp.concatenate([small, jnp.zeros((2, width), f32)])
-    at = 6 * bit
-    qv = every[:, at : at + b_qv.size].reshape(8, 4, *b_qv.shape)
-    at += b_qv.size
-    ups = every[:, at : at + b_up.size].reshape(8, 4, *b_up.shape)
-    at += b_up.size
-    first = every[:, at : at + 4].reshape(8, 4, 4)[:, 0]
-    starts_row = lax.dynamic_index_in_dim(first, 2 * z + y, 0, keepdims=False).astype(jnp.int32)
-    qv = qv.transpose(1, 2, 0, 3).reshape(4, 4, b_qv.shape[0] // 4, 8 * b_qv.shape[1])
-    qv = lax.dynamic_index_in_dim(qv, member, 1, keepdims=False).reshape(4, 2, dim)
-    bq = jnp.stack([qv[:, 0], jnp.zeros_like(qv[:, 0]), qv[:, 1]]).reshape(1, 3 * 4 * dim)
-    ups = ups.transpose(1, 2, 0, 3).reshape(4, 4, b_up.shape[0] // 4, 8 * b_up.shape[1])
-    bu = lax.dynamic_index_in_dim(ups, member, 1, keepdims=False).reshape(1, 4 * hidden)
-    in_q = w_qkv.reshape(part, 4, 3, dim).transpose(1, 2, 3, 0)
+    here = jnp.arange(part) // bit == z
+    vectors = jnp.stack([ln1_gain, ln1_bias, b_out, ln2_gain, ln2_bias, b_down])
+    vectors = jnp.where(here, jnp.tile(vectors, (1, part // bit)), 0.0)
+    begins = jnp.where(z == 0, starts.astype(f32), 0.0)
+    begins = jnp.pad(begins, ((0, 1), (0, part - 4)))
+    spot = (jnp.arange(8) == dp)[:, None]
+
+    def spread(bias):
+        entries = bias.astype(f32).reshape(4, -1, 1, bias.shape[1])
+        return jnp.where(spot, entries, 0.0).reshape(4, -1, part)
+
+    biases = jnp.concatenate(
+        [spread(b_qv), spread(b_up), jnp.zeros((4, 5, part), f32)], axis=1
+    )
+    si = jnp.concatenate([jnp.concatenate([vectors, begins])[None], biases])
+    in_q = w_qkv.reshape(part, 4, 3 * dim).transpose(1, 2, 0)
     in_o = w_out.reshape(4, dim, part)
     in_d = w_down.reshape(4, hidden, part)
-    out, gtok, eq, eo, eu, ed, sums, bsum = fused_layer(
-        starts_row, tokens_in, grad_out, in_q, in_o, w_up, in_d, small, bq, bu
-    )
-    grad_w_qkv = eq.transpose(3, 0, 1, 2).reshape(part, 3 * 4 * dim).astype(f32)
+    out, gtok, eq, eo, eu, ed, fs, fb = fused_layer(
+        tokens_in, grad_out, in_q, in_o, w_up, in_d, si
+    )
+    grad_w_qkv = eq.transpose(2, 0, 1).reshape(part, 3 * 4 * dim).astype(f32)
     grad_w_out = eo.reshape(4 * dim, part).astype(f32)
     grad_w_up = eu.transpose(1, 0, 2).reshape(part, 4 * hidden).astype(f32)
     grad_w_down = ed.reshape(4 * hidden, part).astype(f32)
-    up_sum = bsum[0, : 4 * hidden].reshape(4, 1, hidden)
-    qv_sum = bsum[1, : 3 * 4 * dim].reshape(3, 4, dim)
-    qv_sum = jnp.stack([qv_sum[0], qv_sum[2]], axis=1).reshape(4, 1, 2 * dim)
-    spot = (jnp.arange(4) == member)[None, :, None]
-    up_sum = jnp.where(spot, up_sum, 0.0)
-    qv_sum = jnp.where(spot, qv_sum, 0.0)
-    up_sum = up_sum.reshape(4, 4, b_up.shape[0] // 4, 8, b_up.shape[1]).transpose(3, 0, 1, 2, 4)
-    qv_sum = qv_sum.reshape(4, 4, b_qv.shape[0] // 4, 8, b_qv.shape[1]).transpose(3, 0, 1, 2, 4)
-    vectors = sums[:6].reshape(6, 32, bit).transpose(1, 0, 2).reshape(32, 6 * bit)
-    joined = jnp.concatenate(
-        [vectors, qv_sum.reshape(32, b_qv.size), up_sum.reshape(32, b_up.size)], axis=1
-    )
-    mine = lax.psum_scatter(joined, ("dp", "tensor"), scatter_dimension=0, tiled=True)[0]
-    take = [mine[k * bit : (k + 1) * bit] for k in range(6)]
-    at = 6 * bit
-    grad_b_qv = mine[at : at + b_qv.size].reshape(b_qv.shape)
-    grad_b_up = mine[at + b_qv.size :].reshape(b_up.shape)
+    take = lax.dynamic_slice_in_dim(fs, z * bit, bit, 1)
+
+    def collect(rows, like):
+        entries = rows.reshape(4, -1, 8, like.shape[1])
+        return lax.dynamic_index_in_dim(entries, dp, 2, keepdims=False).reshape(like.shape)
+
+    grad_b_qv = collect(fb[:, 0], b_qv)
+    grad_b_up = collect(fb[:, 1:3], b_up)
     return (
         out, gtok, take[0], take[1], grad_w_qkv, grad_b_qv, grad_w_out, take[2],
         take[3], take[4], grad_w_up, grad_b_up, grad_w_down, take[5],

time: 423 us -> 324 us (0.77)
  blocking collectives: 115 us -> 0 us
  Pallas kernels: 281 us -> 305 us
  local copies, waits for them, and re-layouts: 21.1 us -> 12.8 us
    all_gather x1 -> x0, blocking collectives: 64.9 us -> none  [per_device_fused(): every = lax.all_gather(packed, ('dp', 'tensor'), axis=0, tiled=True)]
    unnamed x1 -> x0, blocking collectives: 50.3 us -> none
    pallas_call x1, Pallas kernels: 281 us -> 305 us  [fused_layer(): pl.pallas_call(kernel, out_shape=(jax.ShapeDtypeStruct((rows, width), low...]
    unnamed x49 -> x39, local copies, waits for them, and re-layouts: 11.9 us -> 7.65 us
where the time goes in v2:
time: 324 us; the launch traced here: 321 us
  Pallas kernels  305 us (94%)
  local copies, waits for them, and re-layouts  12.8 us (4%)
    pallas_call x1, Pallas kernels, fused_layer(): pl.pallas_call(kernel, out_shape=(jax.ShapeDtypeStruct((rows, width), low...  305 us
    unnamed x39, local copies, waits for them, and re-layouts  7.65 us

profile of v2, /device:TPU:1, one launch (start us, length us, event | category | flops | bytes accessed | tf_op | source)
XLA Modules:
  0.0 321.0 jit_solution(11531571872823876185)
XLA Ops:
  0.7 0.0 copy-start.16
  0.7 0.6 copy-done.16
  1.3 0.0 copy-start.8
  1.3 0.0 copy-start.9
  1.4 0.0 copy-start.10
  1.4 0.0 copy-start.11
  1.4 0.0 copy-start.12
  1.4 0.0 copy-start.13
  1.4 0.1 pad.8.clone
  1.5 0.5 copy-done.8
  2.0 0.0 copy-done.9
  2.0 0.0 copy-done.10
  2.0 0.0 copy-done.11
  2.0 0.0 copy-done.12
  2.1 0.0 copy-done.13
  2.1 0.0 copy-start.14
  2.1 0.6 copy-done.14
  2.7 0.1 reshape.112
  2.8 0.0 copy-start.15
  2.8 0.1 copy.36
  2.9 0.6 copy-done.15
  3.5 0.1 reshape.113
  3.6 0.1 tile.10
  3.7 0.1 broadcast_in_dim.85
  3.7 0.1 broadcast_in_dim.86
  3.9 0.1 copy.38
  4.0 0.1 broadcast_in_dim.93
  4.1 0.2 broadcast_in_dim.94
  4.2 0.0 copy-start.4
  4.3 0.1 copy.37
  4.3 0.1 broadcast_in_dim.98
  4.4 0.1 copy.39
  4.5 0.7 maximum_maximum_fusion.refs_6_
  5.2 0.0 copy-done.4
  5.2 0.8 copy.35
  6.0 305.0 %fused_layer.1 = (bf16[256,1024]{1,0:T(8,128)(2,1)}, bf16[256,1024]{1,0:T(8,128)(2,1)}, bf16[4,192,128]{2,1,0:T(8,128)(2,1)}, bf16[4,64,128]{2,1,0:T(8,128)(2,1)...) custom-call(bf16[256,1024]{1,0:T(8,128)(2,1)} %refs_0_.1, ...), custom_call_target="tpu_custom_call" | custom-call | tf_op jit(solution)/shard_map/fused_layer/pallas_call | solution.py:1319
  311.0 0.7 slice.26
  311.7 0.0 copy-start.7
  311.7 0.7 slice.30
  312.4 0.0 copy-done.7
  312.4 0.1 constant_dynamic-slice_fusion.2
  312.5 0.5 slice_bitcast_fusion
  313.0 0.1 copy.40
  313.2 0.1 copy.41
  313.2 0.0 copy-start.6
  313.2 0.6 reshape.109
  313.9 0.1 copy.43
  314.1 0.1 copy.44
  314.2 0.6 reshape.111
  314.8 0.0 copy-done.6
  314.8 0.7 bitcast_convert_fusion.1
  315.5 0.0 copy-done.5
  315.5 0.0 copy-start.3
  315.5 0.9 copy.45
  316.4 0.0 copy-done.3
  316.5 0.2 copy.42
  316.7 0.0 copy-start.2
  316.7 1.0 copy.46
  317.7 0.0 copy-done.2
  317.7 0.8 bitcast_convert_fusion
  318.6 0.4 copy-done.1
  318.9 0.8 copy.49
  319.7 0.4 copy-done
  320.2 0.8 copy.50
  (18 shorter events, 0.2 us)
Async XLA Ops:
  0.7 0.7 copy-start.16
  1.3 0.7 copy-start.8
  1.3 0.7 copy-start.9
  1.4 0.7 copy-start.10
  1.4 0.7 copy-start.11
  1.4 0.7 copy-start.12
  1.4 0.7 copy-start.13
  2.1 0.7 copy-start.14
  2.8 0.7 copy-start.15
  4.2 0.9 copy-start.4
  311.7 0.7 copy-start.7
  313.2 1.6 copy-start.6
  313.9 1.6 copy-start.5
  315.5 1.0 copy-start.3
  316.7 1.0 copy-start.2
  317.7 1.2 copy-start.1
  318.9 1.2 copy-start

commit v3 on v2

--- a/solution.py
+++ b/solution.py
@@ -343,6 +343,7 @@
 
 MESH = pl.DeviceIdType.MESH
 CH = 2
+HOPS = 4
 
 
 class Fused:
@@ -415,7 +416,7 @@
             if when is None:
                 copy.wait_send()
             else:
-                pl.when(when)(copy.wait_send)
+                pl.when(when())(copy.wait_send)
 
     def at_quarter(self, quarter, chunk=None):
         if chunk is None:
@@ -480,6 +481,56 @@
         @pl.when(same)
         def _():
             local.wait()
+
+    def hop_rows(self, chunk):
+        size = self.rows // HOPS
+        return pl.ds(chunk * size, size)
+
+    def hop_one(self, src, mid, index):
+        plane = 2 * self.y + self.x
+        member = (plane + self.z) % 4
+        first = self.dev(self.c, member % 2, member // 2, self.z)
+        same = (self.c == self.y) & (member % 2 == self.x) & (member // 2 == self.c)
+        for chunk in range(HOPS):
+            view, there = src.at[self.hop_rows(chunk)], mid.at[self.hop_rows(chunk)]
+            copy = self.copy(view, there, first, index + chunk)
+            local = pltpu.make_async_copy(view, there, self.lsem.at[index + chunk])
+            pl.when(jnp.logical_not(same))(copy.start)
+            pl.when(same)(local.start)
+
+    def hop_two(self, src, mid, dst, place, index, onward):
+        plane = (self.j - self.z + 4) % 4
+        member = (2 * self.y + self.x + self.z) % 4
+        home = (self.c == self.y) & (member % 2 == self.x) & (member // 2 == self.c)
+        stay = plane == self.z
+        for chunk in range(HOPS):
+            rows = self.hop_rows(chunk)
+            size = self.rows // HOPS
+            there = dst.at[pl.ds(pl.multiple_of(place + chunk * size, size), size)]
+            first = self.copy(src.at[rows], mid.at[rows], self.sib, index + chunk)
+            local = pltpu.make_async_copy(src.at[rows], mid.at[rows], self.lsem.at[index + chunk])
+            pl.when(jnp.logical_not(home))(first.wait_send)
+            pl.when(jnp.logical_not(home))(first.wait_recv)
+            pl.when(home)(local.wait)
+            copy = self.copy(
+                mid.at[rows], there, self.dev(self.y, self.x, self.c, plane), onward + chunk
+            )
+            keep = pltpu.make_async_copy(mid.at[rows], there, self.lsem.at[onward + chunk])
+            pl.when(jnp.logical_not(stay))(copy.start)
+            pl.when(stay)(keep.start)
+
+    def hop_wait(self, mid, dst, place, onward):
+        plane = (self.j - self.z + 4) % 4
+        stay = plane == self.z
+        for chunk in range(HOPS):
+            rows = self.hop_rows(chunk)
+            size = self.rows // HOPS
+            there = dst.at[pl.ds(pl.multiple_of(place + chunk * size, size), size)]
+            copy = self.copy(mid.at[rows], there, self.sib, onward + chunk)
+            keep = pltpu.make_async_copy(mid.at[rows], there, self.lsem.at[onward + chunk])
+            pl.when(jnp.logical_not(stay))(copy.wait_send)
+            pl.when(jnp.logical_not(stay))(copy.wait_recv)
+            pl.when(stay)(keep.wait)
 
     def span(self, half):
         return pl.ds(pl.multiple_of(half * 4 * self.part, 4 * self.part), 4 * self.part)
@@ -530,14 +581,14 @@
         for view, index in self.one[kind]:
             self.arrived(view, index)
         here = self.mine(kind, self.z)
-        for step, when in ((2, None), (1, self.z != 3), (3, self.z != 0)):
+        for step, when in ((2, None), (1, lambda: self.z != 3), (3, lambda: self.z != 0)):
             plane = (self.z + step) % 4
             index = self.two[kind] + step
             copy = self.copy(here, here, self.dev(self.y, self.x, self.c, plane), index)
             if when is None:
                 copy.start()
             else:
-                pl.when(when)(copy.start)
+                pl.when(when())(copy.start)
             self.later(lambda: self.mine(kind, self.z), index, when)
 
     def weights_relay(self, kind, guard=None):
@@ -555,7 +606,9 @@
 
     def relayed(self, kind):
         self.later(
-            lambda: self.mine(kind, self.z), self.pass_sem[kind], (self.z == 1) | (self.z == 2)
+            lambda: self.mine(kind, self.z),
+            self.pass_sem[kind],
+            lambda: (self.z == 1) | (self.z == 2),
         )
         for step in range(4):
             self.later(lambda: self.mine(kind, self.z), self.three[kind] + step)
@@ -862,25 +915,19 @@
         self.barrier()
         move = [self.sem() for _ in range(4)]
         self.small_one()
-        self.move_start(self.tok, self.xs, True, move[0])
-        for kind in "qoud":
-            self.weights_one(kind)
+        hop = [self.sem(HOPS) for _ in range(4)]
+        self.hop_one(self.tok, self.mid_x, hop[0])
+        self.weights_one("q")
         plan_one, plan_two, plan_go, plan_mid = (self.gather_plan() for _ in range(4))
-        self.weights_two("q")
-        self.weights_cross("q", 0)
+        self.hop_two(self.tok, self.mid_x, self.xs, 0, hop[0], hop[1])
         self.small_two()
-        for kind in "ou":
-            self.weights_two(kind)
-        landed = pl.ds(pl.multiple_of(self.z * rows, rows), rows)
         own_rows = self.at_quarter(self.q)
-        self.move_start(self.go, self.gg.at[landed], True, move[1])
-        self.weights_two("d")
         self.small_three()
         gain_one, shift_one = self.small[0:1, :], self.small[1:2, :]
         bias_out = self.small[2:3, :]
         gain_two, shift_two = self.small[3:4, :], self.small[4:5, :]
         bias_down = self.small[5:6, :]
-        self.move_wait(self.tok, self.xs, move[0])
+        self.hop_wait(self.mid_x, self.xs, 0, hop[1])
 
         for chunk in range(CH):
             part = self.at_chunk(chunk)
@@ -889,9 +936,13 @@
             self.i1[part, :] = inverse
             self.h1[self.at_quarter(self.q, chunk), :] = (normed * gain_one + shift_one).astype(low)
             self.gather_send(self.h1, plan_one, chunk)
+        self.weights_two("q")
+        self.weights_cross("q", 0)
         self.mask_blocks()
         self.gather_sib(self.h1, plan_one)
         self.gather_pass(self.h1, plan_one)
+        for kind in "oud":
+            self.weights_one(kind)
         self.gather_last(self.h1, plan_one)
 
         def parts_of(block):
@@ -927,14 +978,16 @@
                 self.weights_relay("q", step == 0)
                 self.weights_cross("q", coming)
 
-            @pl.when(step == 2)
+            @pl.when(step == 1)
+            def _():
+                self.weights_two("o")
+                self.weights_two("u")
+                self.hop_one(self.go, self.ox, hop[2])
+
+            @pl.when(step == 3)
             def _():
                 self.weights_start_three("o")
                 self.weights_three("o")
-
-            @pl.when(step == 3)
-            def _():
-                self.weights_start_three("u")
 
             for block in quarters:
                 place = pl.ds(block * rows, rows)
@@ -988,6 +1041,8 @@
             0,
             self.rx.at[0],
         )
+        self.weights_start_three("u")
+        self.hop_two(self.go, self.ox, self.gg, self.z * rows, hop[2], hop[3])
         self.weights_three("u")
         for chunk in range(CH):
             part = self.at_chunk(chunk)
@@ -999,12 +1054,8 @@
             self.i2[part, :] = inverse
             self.h2[self.at_quarter(self.q, chunk), :] = (normed * gain_two + shift_two).astype(low)
             self.gather_send(self.h2, plan_two, chunk)
-        self.move_wait(self.go, self.gg.at[landed], move[1])
-        for chunk in range(CH):
-            self.gather_send(self.gg, plan_go, chunk)
+        self.weights_two("d")
         self.weights_done("u")
-        self.weights_start_three("d")
-        self.relayed("d")
 
         def up(quarter):
             place = self.at_quarter(quarter)
@@ -1025,26 +1076,35 @@
 
         self.gathered(self.h2, plan_two, up)
 
+        self.hop_wait(self.ox, self.gg, self.q * rows, hop[3])
+        for chunk in range(CH):
+            self.gather_send(self.gg, plan_go, chunk)
+        flat_down = lambda: self.wd[...].reshape(4 * hidden, width)
+        self.weights_start_three("d")
+        self.relayed("d")
         self.weights_three("d")
+        self.gather_sib(self.gg, plan_go)
+        self.gather_pass(self.gg, plan_go)
+        grad_out = self.gg[own_rows, :].astype(f32)
+        self.sums[5:6, :] = jnp.sum(grad_out, axis=0, keepdims=True)
+        self.gather_last(self.gg, plan_go)
+
+        def down_grad(block, carry):
+            lanes = pl.ds(pl.multiple_of(block * hidden, hidden), hidden)
+            self.dd[block] = dot_first(self.hid[:, lanes], self.gg[...]).astype(low)
+            return carry
+
+        lax.fori_loop(0, 4, down_grad, 0)
+        self.grads_one("d")
         self.weights_done("d")
-        flat_down = lambda: self.wd[...].reshape(4 * hidden, width)
-        started_down = self.scatter_start(
-            lambda quarter: jnp.dot(
-                self.hid[self.at_quarter(quarter), :], flat_down(), preferred_element_type=f32
-            ),
-            self.own_b,
-            1,
-            self.rx.at[1],
-        )
 
         def to_up(quarter):
             place = self.at_quarter(quarter)
             value = dot_last(self.gg[place, :], flat_down())
             self.gu[place, :] = (self.gu[place, :].astype(f32) * value).astype(low)
 
-        self.gathered(self.gg, plan_go, to_up)
-        grad_out = self.gg[own_rows, :].astype(f32)
-        self.sums[5:6, :] = jnp.sum(grad_out, axis=0, keepdims=True)
+        for quarter in (self.q_d, self.q_x, self.q_sib, self.q):
+            to_up(quarter)
 
         def two_part(quarter):
             place = self.at_quarter(quarter)
@@ -1055,13 +1115,6 @@
 
         started = self.scatter_start(two_part, self.own_a, 0, self.rx.at[0])
 
-        def down_grad(block, carry):
-            lanes = pl.ds(pl.multiple_of(block * hidden, hidden), hidden)
-            self.dd[block] = dot_first(self.hid[:, lanes], self.gg[...]).astype(low)
-            return carry
-
-        lax.fori_loop(0, 4, down_grad, 0)
-        self.grads_one("d")
         step = width // 4
 
         def up_grad(block, carry):
@@ -1095,13 +1148,6 @@
             self.cb[place // 2, 1 + place % 2 : 2 + place % 2, :] = up_sum[
                 :, place * lanes : (place + 1) * lanes
             ]
-        for chunk in range(CH):
-            part = self.at_chunk(chunk)
-            summed = self.scatter_chunk(started_down, self.own_b, chunk)
-            self.ox[part, :] = (self.mid[part, :] + summed + bias_down).astype(low)
-        self.move_start(self.ox, self.out, False, move[2])
-        self.grads_two("d")
-
         def to_heads(quarter):
             place = self.at_quarter(quarter)
             value = dot_last(self.ga[place, :], flat_out()).astype(low)
@@ -1109,7 +1155,15 @@
                 self.hh[head, place, :] = value[:, head * dim : (head + 1) * dim]
 
         self.gathered(self.ga, plan_mid, to_heads)
-        self.grads_two("u")
+        self.grads_two("d")
+        started_down = self.scatter_start(
+            lambda quarter: jnp.dot(
+                self.hid[self.at_quarter(quarter), :], flat_down(), preferred_element_type=f32
+            ),
+            self.own_b,
+            1,
+            self.rx.at[1],
+        )
         self.do[...] = dot_first(self.ho[...], self.ga[...]).astype(low).reshape(self.do.shape)
         self.grads_one("o")
 
@@ -1155,6 +1209,14 @@
                 self.head_add(step - 1, before)
                 self.head_two(step - 1, before)
 
+            @pl.when(step == 1)
+            def _():
+                for chunk in range(CH):
+                    part = self.at_chunk(chunk)
+                    summed = self.scatter_chunk(started_down, self.own_b, chunk)
+                    self.ox[part, :] = (self.mid[part, :] + summed + bias_down).astype(low)
+                self.move_start(self.ox, self.out, False, move[2])
+
             return carry
 
         lax.fori_loop(0, heads, attend_back, 0)
@@ -1163,9 +1225,6 @@
             self.later(lambda: self.cut("q", self.dq, 0, self.span(0)), self.head_y + step)
         for step in range(3):
             self.later(lambda: self.zq.at[0], self.head_z + step)
-        self.grads_three("d")
-        self.grads_three("u")
-        self.grads_two("o")
         started = self.scatter_start(
             lambda quarter: sum(
                 jnp.dot(
@@ -1175,21 +1234,23 @@
                 )
                 for head in range(heads)
             ),
-            self.own_b,
-            1,
-            self.rx.at[2],
-        )
+            self.own_a,
+            0,
+            self.rx.at[0],
+        )
+        self.grads_two("u")
+        self.grads_two("o")
         for head in range(heads):
             total = jnp.sum(self.gp[head].astype(f32), axis=0, keepdims=True)
             self.cb[head, 0:1, 0:dim] = total[:, 0:dim]
             self.cb[head, 0:1, dim:] = total[:, 2 * dim :]
             self.cb[head, 3:, :] = jnp.zeros((5, self.part), f32)
         self.head_add(3, self.z)
-        self.grads_three("o")
+        self.grads_three("d")
         totals = [0.0] * 2
         for chunk in range(CH):
             part = self.at_chunk(chunk)
-            grad_one = self.scatter_chunk(started, self.own_b, chunk)
+            grad_one = self.scatter_chunk(started, self.own_a, chunk)
             normed = self.n1[part, :]
             self.xs[part, :] = (
                 self.gm[part, :] + norm_back(grad_one, normed, self.i1[part, :], gain_one)
@@ -1201,8 +1262,10 @@
         self.sums[6:8, :] = jnp.zeros((2, width), f32)
         self.back_one()
         self.move_start(self.xs, self.gtok, False, move[3])
+        self.grads_three("u")
+        self.grads_three("o")
+        self.back_two()
         self.grads_three("q")
-        self.back_two()
         for kind in "duoq":
             self.grads_done(kind)
         self.move_wait(self.ox, self.out, move[2])
@@ -1243,6 +1306,7 @@
     low, f32 = jnp.bfloat16, jnp.float32
     scratch = dict(
         xs=((rows, width), low),
+        mid_x=((rows, width), low),
         wq=((4, 3 * dim, width), low),
         wo=((4, dim, width), low),
         wu=((4, width, hidden), low),
@@ -1272,7 +1336,7 @@
         gu=((n, 4 * hidden), low),
         ox=((rows, width), low),
         rs=((2, 5, rows, width), low),
-        rx=((3, rows, width), low),
+        rx=((2, rows, width), low),
         dq=((4, 3 * dim, width), low),
         do=((4, dim, width), low),
         du=((4, width, hidden), low),

time: 324 us -> 280 us (0.86)
  Pallas kernels: 305 us -> 263 us
    pallas_call x1, Pallas kernels: 305 us -> 263 us  [fused_layer(): pl.pallas_call(kernel, out_shape=(jax.ShapeDtypeStruct((rows, width), low...]
where the time goes in v3:
time: 280 us; the launch traced here: 279 us
  Pallas kernels  263 us (94%)
  local copies, waits for them, and re-layouts  12.8 us (5%)
    pallas_call x1, Pallas kernels, fused_layer(): pl.pallas_call(kernel, out_shape=(jax.ShapeDtypeStruct((rows, width), low...  263 us
    unnamed x39, local copies, waits for them, and re-layouts  7.65 us

profile of v3, /device:TPU:1, one launch (start us, length us, event | category | flops | bytes accessed | tf_op | source)
XLA Modules:
  0.0 279.0 jit_solution(3871208867321950345)
XLA Ops:
  0.7 0.0 copy-start.16
  0.7 0.6 copy-done.16
  1.3 0.0 copy-start.8
  1.3 0.0 copy-start.9
  1.4 0.0 copy-start.10
  1.4 0.0 copy-start.11
  1.4 0.0 copy-start.12
  1.4 0.0 copy-start.13
  1.4 0.1 pad.8.clone
  1.5 0.5 copy-done.8
  2.0 0.0 copy-done.9
  2.0 0.0 copy-done.10
  2.0 0.0 copy-done.11
  2.0 0.0 copy-done.12
  2.1 0.0 copy-done.13
  2.1 0.0 copy-start.14
  2.1 0.6 copy-done.14
  2.7 0.1 reshape.112
  2.8 0.0 copy-start.15
  2.8 0.1 copy.36
  2.9 0.6 copy-done.15
  3.5 0.1 reshape.113
  3.6 0.1 tile.10
  3.7 0.1 broadcast_in_dim.85
  3.7 0.1 broadcast_in_dim.86
  3.9 0.1 copy.38
  4.0 0.1 broadcast_in_dim.93
  4.1 0.2 broadcast_in_dim.94
  4.2 0.0 copy-start.4
  4.3 0.1 copy.37
  4.3 0.1 broadcast_in_dim.98
  4.4 0.1 copy.39
  4.5 0.7 maximum_maximum_fusion.refs_6_
  5.2 0.0 copy-done.4
  5.2 0.8 copy.35
  6.0 263.0 %fused_layer.1 = (bf16[256,1024]{1,0:T(8,128)(2,1)}, bf16[256,1024]{1,0:T(8,128)(2,1)}, bf16[4,192,128]{2,1,0:T(8,128)(2,1)}, bf16[4,64,128]{2,1,0:T(8,128)(2,1)...) custom-call(bf16[256,1024]{1,0:T(8,128)(2,1)} %refs_0_.1, ...), custom_call_target="tpu_custom_call" | custom-call | tf_op jit(solution)/shard_map/fused_layer/pallas_call | solution.py:1383
  269.0 0.7 slice.26
  269.7 0.7 slice.30
  270.5 0.0 copy-done.7
  270.5 0.1 constant_dynamic-slice_fusion.2
  270.5 0.5 slice_bitcast_fusion
  271.1 0.1 copy.40
  271.2 0.1 copy.41
  271.3 0.0 copy-start.6
  271.3 0.6 reshape.109
  271.9 0.0 copy-start.5
  271.9 0.1 copy.43
  272.1 0.1 copy.44
  272.2 0.6 reshape.111
  272.8 0.0 copy-done.6
  272.8 0.7 bitcast_convert_fusion.1
  273.5 0.0 copy-done.5
  273.6 0.0 copy-start.3
  273.6 0.9 copy.45
  274.5 0.0 copy-done.3
  274.5 0.2 copy.42
  274.7 0.0 copy-start.2
  274.8 1.0 copy.46
  275.7 0.0 copy-done.2
  275.8 0.8 bitcast_convert_fusion
  276.6 0.4 copy-done.1
  277.0 0.8 copy.49
  277.8 0.4 copy-done
  278.2 0.8 copy.50
  (18 shorter events, 0.2 us)
Async XLA Ops:
  0.7 0.7 copy-start.16
  1.3 0.7 copy-start.8
  1.3 0.7 copy-start.9
  1.4 0.7 copy-start.10
  1.4 0.7 copy-start.11
  1.4 0.7 copy-start.12
  1.4 0.7 copy-start.13
  2.1 0.7 copy-start.14
  2.8 0.7 copy-start.15
  4.2 0.9 copy-start.4
  269.7 0.7 copy-start.7
  271.3 1.6 copy-start.6
  271.9 1.6 copy-start.5
  273.6 1.0 copy-start.3
  274.7 1.0 copy-start.2
  275.8 1.2 copy-start.1
  277.0 1.2 copy-start

commit v4 on v3

--- a/solution.py
+++ b/solution.py
@@ -344,6 +344,7 @@
 MESH = pl.DeviceIdType.MESH
 CH = 2
 HOPS = 4
+RELAYED = "ud"
 
 
 class Fused:
@@ -519,10 +520,10 @@
             pl.when(jnp.logical_not(stay))(copy.start)
             pl.when(stay)(keep.start)
 
-    def hop_wait(self, mid, dst, place, onward):
+    def hop_wait(self, mid, dst, place, onward, half):
         plane = (self.j - self.z + 4) % 4
         stay = plane == self.z
-        for chunk in range(HOPS):
+        for chunk in range(half * HOPS // CH, (half + 1) * HOPS // CH):
             rows = self.hop_rows(chunk)
             size = self.rows // HOPS
             there = dst.at[pl.ds(pl.multiple_of(place + chunk * size, size), size)]
@@ -573,15 +574,21 @@
         self.three[kind] = self.sem(4)
         self.pass_sem[kind] = self.sem()
 
-    def mine(self, kind, plane):
-        return self.cut(kind, self.wbuf[kind], plane, self.span(self.y))
-
-    def weights_two(self, kind):
+    def weights_in(self, kind):
         self.own[kind].wait()
         for view, index in self.one[kind]:
             self.arrived(view, index)
+        self.weights_cross(kind, 0)
+
+    def mine(self, kind, plane):
+        return self.cut(kind, self.wbuf[kind], plane, self.span(self.y))
+
+    def weights_two(self, kind):
         here = self.mine(kind, self.z)
-        for step, when in ((2, None), (1, lambda: self.z != 3), (3, lambda: self.z != 0)):
+        near, far = (lambda: self.z != 3), (lambda: self.z != 0)
+        if kind not in RELAYED:
+            near = far = None
+        for step, when in ((2, None), (1, near), (3, far)):
             plane = (self.z + step) % 4
             index = self.two[kind] + step
             copy = self.copy(here, here, self.dev(self.y, self.x, self.c, plane), index)
@@ -592,6 +599,8 @@
             self.later(lambda: self.mine(kind, self.z), index, when)
 
     def weights_relay(self, kind, guard=None):
+        if kind not in RELAYED:
+            return
         for here, plane, step in ((2, 3, 3), (1, 0, 1)):
             when = self.z == here
             block = self.mine(kind, (here + 2) % 4)
@@ -605,11 +614,12 @@
             pl.when(when if guard is None else when & guard)(copy.start)
 
     def relayed(self, kind):
-        self.later(
-            lambda: self.mine(kind, self.z),
-            self.pass_sem[kind],
-            lambda: (self.z == 1) | (self.z == 2),
-        )
+        if kind in RELAYED:
+            self.later(
+                lambda: self.mine(kind, self.z),
+                self.pass_sem[kind],
+                lambda: (self.z == 1) | (self.z == 2),
+            )
         for step in range(4):
             self.later(lambda: self.mine(kind, self.z), self.three[kind] + step)
 
@@ -631,7 +641,6 @@
             self.weights_cross(kind, step)
 
     def weights_start_three(self, kind):
-        self.weights_cross(kind, 0)
         self.weights_here(kind, 2)
         self.weights_relay(kind)
         self.weights_cross(kind, 2)
@@ -648,34 +657,33 @@
             self.weights_ready(kind, step)
 
     def grads_one(self, kind):
-        index = self.sem()
-        self.back[kind] = index
-        for plane in range(4):
+        self.swaps[kind] = [self.sem() for _ in range(3)]
+        for swap in self.swaps[kind]:
+            self.later(lambda: self.zbuf[kind].at[0], swap)
+        for turn in (2, 1, 3, 0):
+            plane = (self.z + turn) % 4
             away = self.cut(kind, self.dbuf[kind], plane, self.span(1 - self.y))
             there = self.cut(kind, self.ybuf[kind], plane, slice(None))
-            use = index if plane == 0 else self.sem()
+            use = self.sem()
             self.send(away, there, self.dev(1 - self.y, self.x, self.c, self.z), use)
-            self.backs.setdefault(kind, []).append(use)
-
-    def grads_two(self, kind):
-        for plane in range(4):
+            self.backs.setdefault(kind, {})[turn] = use
+
+    def grads_two(self, kind, turns=(2, 1, 3, 0)):
+        for turn in turns:
+            plane = (self.z + turn) % 4
             there = self.cut(kind, self.ybuf[kind], plane, slice(None))
-            self.arrived(there, self.backs[kind][plane])
+            self.arrived(there, self.backs[kind][turn])
             mine = self.cut(kind, self.dbuf[kind], plane, self.span(self.y))
             mine[...] = (
                 mine[...].astype(jnp.float32) + there[...].astype(jnp.float32)
             ).astype(jnp.bfloat16)
-        self.swaps[kind] = []
-        for step in range(1, 4):
-            plane = (self.z + step) % 4
-            index = self.sem()
-            self.send(
-                self.cut(kind, self.dbuf[kind], plane, self.span(self.y)),
-                self.zbuf[kind].at[step - 1],
-                self.dev(self.y, self.x, self.c, plane),
-                index,
-            )
-            self.swaps[kind].append(index)
+            if turn:
+                self.copy(
+                    mine,
+                    self.zbuf[kind].at[turn - 1],
+                    self.dev(self.y, self.x, self.c, plane),
+                    self.swaps[kind][turn - 1],
+                ).start()
 
     def head_one(self, step, head):
         self.copy(
@@ -860,7 +868,7 @@
         self.gather_last(buf, plan)
         use(self.q_d)
 
-    def scatter_start(self, partial, own, which, rx):
+    def scatter_start(self, partial, own, which, rx, hold=False):
         sa, ra, sb, sc, rb = (self.rs.at[which, slot] for slot in range(5))
         plan = [[self.sem() for _ in range(CH)] for _ in range(3)]
         low = jnp.bfloat16
@@ -875,15 +883,21 @@
         for chunk in range(CH):
             self.arrived(ra.at[self.at_chunk(chunk)], plan[0][chunk])
         sb[...] = (held + ra[...].astype(jnp.float32)).astype(low)
-        for chunk in range(CH):
-            rows = self.at_chunk(chunk)
-            self.send(sb.at[rows], rx.at[rows], self.across, plan[1][chunk], which)
+        if not hold:
+            self.scatter_send((plan, which, rx))
         sc[...] = partial(self.q_sib).astype(low)
         for chunk in range(CH):
             rows = self.at_chunk(chunk)
             self.send(sc.at[rows], rb.at[rows], self.sib, plan[2][chunk], which)
         own[...] = partial(self.q)
         return plan, which, rx
+
+    def scatter_send(self, started):
+        plan, which, rx = started
+        sb = self.rs.at[which, 2]
+        for chunk in range(CH):
+            rows = self.at_chunk(chunk)
+            self.send(sb.at[rows], rx.at[rows], self.across, plan[1][chunk], which)
 
     def scatter_chunk(self, started, own, chunk):
         plan, which, rx = started
@@ -922,33 +936,37 @@
         self.hop_two(self.tok, self.mid_x, self.xs, 0, hop[0], hop[1])
         self.small_two()
         own_rows = self.at_quarter(self.q)
+        self.weights_in("q")
+        self.weights_two("q")
+        for kind in "ou":
+            self.weights_one(kind)
         self.small_three()
         gain_one, shift_one = self.small[0:1, :], self.small[1:2, :]
         bias_out = self.small[2:3, :]
         gain_two, shift_two = self.small[3:4, :], self.small[4:5, :]
         bias_down = self.small[5:6, :]
-        self.hop_wait(self.mid_x, self.xs, 0, hop[1])
 
         for chunk in range(CH):
             part = self.at_chunk(chunk)
+            self.hop_wait(self.mid_x, self.xs, 0, hop[1], chunk)
             normed, inverse = normalize(self.xs[part, :].astype(f32))
             self.n1[part, :] = normed
             self.i1[part, :] = inverse
             self.h1[self.at_quarter(self.q, chunk), :] = (normed * gain_one + shift_one).astype(low)
             self.gather_send(self.h1, plan_one, chunk)
-        self.weights_two("q")
-        self.weights_cross("q", 0)
         self.mask_blocks()
+        near = 1 + 2 * ((3 - self.z) // 3)
         self.gather_sib(self.h1, plan_one)
+        self.weights_start_three("q")
         self.gather_pass(self.h1, plan_one)
-        for kind in "oud":
-            self.weights_one(kind)
+        self.weights_one("d")
+        self.weights_three("q", (near,))
+        self.weights_in("o")
+        self.weights_two("o")
         self.gather_last(self.h1, plan_one)
 
         def parts_of(block):
             return ([(0, block * rows)] if block else []) + [(block * rows, rows)]
-
-        near = 1 + 2 * ((3 - self.z) // 3)
 
         def turn(step):
             late, odd = step // 2, step % 2
@@ -971,23 +989,24 @@
 
             lax.fori_loop(0, 4, project, 0)
 
-            @pl.when(step < 3)
+            @pl.when(step == 0)
             def _():
-                coming = turn(step + 1)
-                self.weights_here("q", coming)
-                self.weights_relay("q", step == 0)
-                self.weights_cross("q", coming)
+                self.weights_three("q", (4 - near,))
+                self.weights_in("u")
 
             @pl.when(step == 1)
             def _():
-                self.weights_two("o")
+                self.weights_start_three("o")
                 self.weights_two("u")
                 self.hop_one(self.go, self.ox, hop[2])
 
+            @pl.when(step == 2)
+            def _():
+                self.weights_three("o")
+
             @pl.when(step == 3)
             def _():
-                self.weights_start_three("o")
-                self.weights_three("o")
+                self.weights_start_three("u")
 
             for block in quarters:
                 place = pl.ds(block * rows, rows)
@@ -1041,8 +1060,9 @@
             0,
             self.rx.at[0],
         )
-        self.weights_start_three("u")
         self.hop_two(self.go, self.ox, self.gg, self.z * rows, hop[2], hop[3])
+        self.weights_in("d")
+        self.weights_two("d")
         self.weights_three("u")
         for chunk in range(CH):
             part = self.at_chunk(chunk)
@@ -1054,7 +1074,11 @@
             self.i2[part, :] = inverse
             self.h2[self.at_quarter(self.q, chunk), :] = (normed * gain_two + shift_two).astype(low)
             self.gather_send(self.h2, plan_two, chunk)
-        self.weights_two("d")
+        for chunk in range(CH):
+            self.hop_wait(self.ox, self.gg, self.q * rows, hop[3], chunk)
+            self.gather_send(self.gg, plan_go, chunk)
+        self.weights_start_three("d")
+        self.relayed("d")
         self.weights_done("u")
 
         def up(quarter):
@@ -1074,15 +1098,16 @@
                 )
                 self.gu[place, lanes] = slope.astype(low)
 
-        self.gathered(self.h2, plan_two, up)
-
-        self.hop_wait(self.ox, self.gg, self.q * rows, hop[3])
-        for chunk in range(CH):
-            self.gather_send(self.gg, plan_go, chunk)
+        up(self.q)
+        self.gather_sib(self.h2, plan_two)
+        up(self.q_sib)
+        self.weights_three("d", (near,))
+        self.gather_pass(self.h2, plan_two)
+        up(self.q_x)
+        self.weights_three("d", (4 - near,))
+        self.gather_last(self.h2, plan_two)
+        up(self.q_d)
         flat_down = lambda: self.wd[...].reshape(4 * hidden, width)
-        self.weights_start_three("d")
-        self.relayed("d")
-        self.weights_three("d")
         self.gather_sib(self.gg, plan_go)
         self.gather_pass(self.gg, plan_go)
         grad_out = self.gg[own_rows, :].astype(f32)
@@ -1105,6 +1130,7 @@
 
         for quarter in (self.q_d, self.q_x, self.q_sib, self.q):
             to_up(quarter)
+        self.grads_two("d", (2,))
 
         def two_part(quarter):
             place = self.at_quarter(quarter)
@@ -1115,6 +1141,7 @@
 
         started = self.scatter_start(two_part, self.own_a, 0, self.rx.at[0])
 
+        self.grads_two("d", (1,))
         step = width // 4
 
         def up_grad(block, carry):
@@ -1126,6 +1153,16 @@
 
         lax.fori_loop(0, 4, up_grad, 0)
         self.grads_one("u")
+        started_down = self.scatter_start(
+            lambda quarter: jnp.dot(
+                self.hid[self.at_quarter(quarter), :], flat_down(), preferred_element_type=f32
+            ),
+            self.own_b,
+            1,
+            self.rx.at[1],
+            hold=True,
+        )
+        self.grads_two("d", (3, 0))
         totals = [0.0] * 3
         for chunk in range(CH):
             part = self.at_chunk(chunk)
@@ -1142,6 +1179,7 @@
         self.sums[3:4, :] = totals[0]
         self.sums[4:5, :] = totals[1]
         self.sums[2:3, :] = totals[2]
+        self.scatter_send(started_down)
         up_sum = jnp.sum(self.gu[...].astype(f32), axis=0, keepdims=True)
         lanes = self.part
         for place in range(8):
@@ -1154,18 +1192,18 @@
             for head in range(heads):
                 self.hh[head, place, :] = value[:, head * dim : (head + 1) * dim]
 
-        self.gathered(self.ga, plan_mid, to_heads)
-        self.grads_two("d")
-        started_down = self.scatter_start(
-            lambda quarter: jnp.dot(
-                self.hid[self.at_quarter(quarter), :], flat_down(), preferred_element_type=f32
-            ),
-            self.own_b,
-            1,
-            self.rx.at[1],
-        )
+        to_heads(self.q)
+        self.gather_sib(self.ga, plan_mid)
+        to_heads(self.q_sib)
+        self.grads_two("u", (2,))
+        self.gather_pass(self.ga, plan_mid)
+        to_heads(self.q_x)
+        self.grads_two("u", (1,))
+        self.gather_last(self.ga, plan_mid)
+        to_heads(self.q_d)
         self.do[...] = dot_first(self.ho[...], self.ga[...]).astype(low).reshape(self.do.shape)
         self.grads_one("o")
+        self.grads_two("u", (3, 0))
 
         self.head_y, self.head_z = self.sem(4), self.sem(3)
 
@@ -1203,11 +1241,9 @@
             self.dq[head] = dot_first(self.gp[head], self.h1[...]).astype(low)
             self.head_one(step, head)
 
-            @pl.when(step > 0)
+            @pl.when(step == 2)
             def _():
-                before = (self.z + step) % 4
-                self.head_add(step - 1, before)
-                self.head_two(step - 1, before)
+                self.grads_two("o")
 
             @pl.when(step == 1)
             def _():
@@ -1238,15 +1274,17 @@
             0,
             self.rx.at[0],
         )
-        self.grads_two("u")
-        self.grads_two("o")
+        for step in range(3):
+            head = (self.z + 1 + step) % 4
+            self.head_add(step, head)
+            self.head_two(step, head)
         for head in range(heads):
             total = jnp.sum(self.gp[head].astype(f32), axis=0, keepdims=True)
             self.cb[head, 0:1, 0:dim] = total[:, 0:dim]
             self.cb[head, 0:1, dim:] = total[:, 2 * dim :]
             self.cb[head, 3:, :] = jnp.zeros((5, self.part), f32)
+        self.grads_three("d")
         self.head_add(3, self.z)
-        self.grads_three("d")
         totals = [0.0] * 2
         for chunk in range(CH):
             part = self.at_chunk(chunk)

time: 280 us -> 239 us (0.85)
  Pallas kernels: 263 us -> 222 us
    pallas_call x1, Pallas kernels: 263 us -> 222 us  [fused_layer(): pl.pallas_call(kernel, out_shape=(jax.ShapeDtypeStruct((rows, width), low...]
where the time goes in v4:
time: 239 us; the launch traced here: 238 us
  Pallas kernels  222 us (93%)
  local copies, waits for them, and re-layouts  12.8 us (5%)
    pallas_call x1, Pallas kernels, fused_layer(): pl.pallas_call(kernel, out_shape=(jax.ShapeDtypeStruct((rows, width), low...  222 us
    unnamed x39, local copies, waits for them, and re-layouts  7.65 us

profile of v4, /device:TPU:1, one launch (start us, length us, event | category | flops | bytes accessed | tf_op | source)
XLA Modules:
  0.0 238.3 jit_solution(5725483822424822944)
XLA Ops:
  0.7 0.0 copy-start.16
  0.7 0.6 copy-done.16
  1.3 0.0 copy-start.8
  1.3 0.0 copy-start.9
  1.4 0.0 copy-start.10
  1.4 0.0 copy-start.11
  1.4 0.0 copy-start.12
  1.4 0.0 copy-start.13
  1.4 0.1 pad.8.clone
  1.5 0.5 copy-done.8
  2.0 0.0 copy-done.9
  2.0 0.0 copy-done.10
  2.0 0.0 copy-done.11
  2.0 0.0 copy-done.12
  2.1 0.0 copy-done.13
  2.1 0.0 copy-start.14
  2.1 0.6 copy-done.14
  2.7 0.1 reshape.112
  2.8 0.0 copy-start.15
  2.8 0.1 copy.36
  2.9 0.6 copy-done.15
  3.5 0.1 reshape.113
  3.6 0.1 tile.10
  3.7 0.1 broadcast_in_dim.85
  3.7 0.1 broadcast_in_dim.86
  3.9 0.1 copy.38
  4.0 0.1 broadcast_in_dim.93
  4.1 0.2 broadcast_in_dim.94
  4.2 0.0 copy-start.4
  4.3 0.1 copy.37
  4.3 0.1 broadcast_in_dim.98
  4.4 0.1 copy.39
  4.5 0.7 maximum_maximum_fusion.refs_6_
  5.2 0.0 copy-done.4
  5.2 0.8 copy.35
  6.0 222.3 %fused_layer.1 = (bf16[256,1024]{1,0:T(8,128)(2,1)}, bf16[256,1024]{1,0:T(8,128)(2,1)}, bf16[4,192,128]{2,1,0:T(8,128)(2,1)}, bf16[4,64,128]{2,1,0:T(8,128)(2,1)...) custom-call(bf16[256,1024]{1,0:T(8,128)(2,1)} %refs_0_.1, ...), custom_call_target="tpu_custom_call" | custom-call | tf_op jit(solution)/shard_map/fused_layer/pallas_call | solution.py:1421
  228.3 0.7 slice.26
  229.0 0.7 slice.30
  229.7 0.0 copy-done.7
  229.7 0.1 constant_dynamic-slice_fusion.2
  229.8 0.5 slice_bitcast_fusion
  230.3 0.1 copy.40
  230.4 0.1 copy.41
  230.5 0.0 copy-start.6
  230.5 0.6 reshape.109
  231.2 0.0 copy-start.5
  231.2 0.1 copy.43
  231.3 0.1 copy.44
  231.4 0.6 reshape.111
  232.1 0.0 copy-done.6
  232.1 0.7 bitcast_convert_fusion.1
  232.8 0.0 copy-done.5
  232.8 0.0 copy-start.3
  232.8 0.9 copy.45
  233.7 0.0 copy-done.3
  233.8 0.2 copy.42
  234.0 0.0 copy-start.2
  234.0 1.0 copy.46
  235.0 0.0 copy-done.2
  235.0 0.8 bitcast_convert_fusion
  235.8 0.4 copy-done.1
  236.2 0.8 copy.49
  237.0 0.4 copy-done
  237.5 0.8 copy.50
  (18 shorter events, 0.2 us)
Async XLA Ops:
  0.7 0.7 copy-start.16
  1.3 0.7 copy-start.8
  1.3 0.7 copy-start.9
  1.4 0.7 copy-start.10
  1.4 0.7 copy-start.11
  1.4 0.7 copy-start.12
  1.4 0.7 copy-start.13
  2.1 0.7 copy-start.14
  2.8 0.7 copy-start.15
  4.2 0.9 copy-start.4
  229.0 0.7 copy-start.7
  230.5 1.6 copy-start.6
  231.2 1.6 copy-start.5
  232.8 1.0 copy-start.3
  234.0 1.0 copy-start.2
  235.0 1.2 copy-start.1
  236.2 1.2 copy-start

commit v5 on v4

--- a/solution.py
+++ b/solution.py
@@ -381,7 +381,7 @@
         return self.dev(self.y, member % 2, member // 2, self.z)
 
     def quarter(self, member):
-        return (member - self.z + 4) % 4
+        return (member - self.z - self.y + 8) % 4
 
     def sem(self, count=1):
         index = self.next_sem
@@ -445,7 +445,7 @@
 
     def homes(self):
         plane = 2 * self.y + self.x
-        member = (plane + self.z) % 4
+        member = (plane + self.z + self.c) % 4
         worker = (self.c, member % 2, member // 2, plane)
         owner = (self.z // 2, self.z % 2, self.y, self.q)
         same = (
@@ -489,7 +489,7 @@
 
     def hop_one(self, src, mid, index):
         plane = 2 * self.y + self.x
-        member = (plane + self.z) % 4
+        member = (plane + self.z + self.c) % 4
         first = self.dev(self.c, member % 2, member // 2, self.z)
         same = (self.c == self.y) & (member % 2 == self.x) & (member // 2 == self.c)
         for chunk in range(HOPS):
@@ -500,8 +500,8 @@
             pl.when(same)(local.start)
 
     def hop_two(self, src, mid, dst, place, index, onward):
-        plane = (self.j - self.z + 4) % 4
-        member = (2 * self.y + self.x + self.z) % 4
+        plane = self.q
+        member = (2 * self.y + self.x + self.z + self.c) % 4
         home = (self.c == self.y) & (member % 2 == self.x) & (member // 2 == self.c)
         stay = plane == self.z
         for chunk in range(HOPS):
@@ -521,7 +521,7 @@
             pl.when(stay)(keep.start)
 
     def hop_wait(self, mid, dst, place, onward, half):
-        plane = (self.j - self.z + 4) % 4
+        plane = self.q
         stay = plane == self.z
         for chunk in range(half * HOPS // CH, (half + 1) * HOPS // CH):
             rows = self.hop_rows(chunk)
@@ -842,8 +842,9 @@
 
     def gather_send(self, buf, plan, chunk):
         rows = self.at_quarter(self.q, chunk)
-        self.send(buf.at[rows], buf.at[rows], self.across, plan["across"][chunk])
-        self.send(buf.at[rows], buf.at[rows], self.sib, plan["sib"][chunk])
+        for device, kind in ((self.across, "across"), (self.sib, "sib")):
+            self.copy(buf.at[rows], buf.at[rows], device, plan[kind][chunk]).start()
+            self.later(lambda: buf.at[self.at_quarter(self.q, 0)], plan[kind][chunk])
 
     def gather_pass(self, buf, plan):
         for chunk in range(CH):
@@ -931,6 +932,7 @@
         self.small_one()
         hop = [self.sem(HOPS) for _ in range(4)]
         self.hop_one(self.tok, self.mid_x, hop[0])
+        self.hop_one(self.go, self.ox, hop[2])
         self.weights_one("q")
         plan_one, plan_two, plan_go, plan_mid = (self.gather_plan() for _ in range(4))
         self.hop_two(self.tok, self.mid_x, self.xs, 0, hop[0], hop[1])
@@ -958,11 +960,12 @@
         near = 1 + 2 * ((3 - self.z) // 3)
         self.gather_sib(self.h1, plan_one)
         self.weights_start_three("q")
+        self.weights_in("o")
+        self.weights_two("o")
+        self.hop_two(self.go, self.ox, self.gg, self.z * rows, hop[2], hop[3])
         self.gather_pass(self.h1, plan_one)
         self.weights_one("d")
         self.weights_three("q", (near,))
-        self.weights_in("o")
-        self.weights_two("o")
         self.gather_last(self.h1, plan_one)
 
         def parts_of(block):
@@ -993,16 +996,18 @@
             def _():
                 self.weights_three("q", (4 - near,))
                 self.weights_in("u")
+                self.weights_two("u")
 
             @pl.when(step == 1)
             def _():
                 self.weights_start_three("o")
-                self.weights_two("u")
-                self.hop_one(self.go, self.ox, hop[2])
 
             @pl.when(step == 2)
             def _():
                 self.weights_three("o")
+                for chunk in range(CH):
+                    self.hop_wait(self.ox, self.gg, self.q * rows, hop[3], chunk)
+                    self.gather_send(self.gg, plan_go, chunk)
 
             @pl.when(step == 3)
             def _():
@@ -1060,7 +1065,6 @@
             0,
             self.rx.at[0],
         )
-        self.hop_two(self.go, self.ox, self.gg, self.z * rows, hop[2], hop[3])
         self.weights_in("d")
         self.weights_two("d")
         self.weights_three("u")
@@ -1074,9 +1078,8 @@
             self.i2[part, :] = inverse
             self.h2[self.at_quarter(self.q, chunk), :] = (normed * gain_two + shift_two).astype(low)
             self.gather_send(self.h2, plan_two, chunk)
-        for chunk in range(CH):
-            self.hop_wait(self.ox, self.gg, self.q * rows, hop[3], chunk)
-            self.gather_send(self.gg, plan_go, chunk)
+        self.gather_sib(self.gg, plan_go)
+        self.gather_pass(self.gg, plan_go)
         self.weights_start_three("d")
         self.relayed("d")
         self.weights_done("u")
@@ -1108,8 +1111,6 @@
         self.gather_last(self.h2, plan_two)
         up(self.q_d)
         flat_down = lambda: self.wd[...].reshape(4 * hidden, width)
-        self.gather_sib(self.gg, plan_go)
-        self.gather_pass(self.gg, plan_go)
         grad_out = self.gg[own_rows, :].astype(f32)
         self.sums[5:6, :] = jnp.sum(grad_out, axis=0, keepdims=True)
         self.gather_last(self.gg, plan_go)
@@ -1203,7 +1204,6 @@
         to_heads(self.q_d)
         self.do[...] = dot_first(self.ho[...], self.ga[...]).astype(low).reshape(self.do.shape)
         self.grads_one("o")
-        self.grads_two("u", (3, 0))
 
         self.head_y, self.head_z = self.sem(4), self.sem(3)
 
@@ -1240,6 +1240,10 @@
             self.gp[head, :, 2 * dim :] = self.va[...].astype(low)
             self.dq[head] = dot_first(self.gp[head], self.h1[...]).astype(low)
             self.head_one(step, head)
+
+            @pl.when(step == 0)
+            def _():
+                self.grads_two("u", (3, 0))
 
             @pl.when(step == 2)
             def _():
@@ -1442,6 +1446,66 @@
     )(tok, go, in_q, in_o, in_u, in_d, si)
 
 
+def finish(out, gtok, eq, eo, eu, ed, fs, fb):
+    rows, width = out.shape
+    part = eq.shape[2]
+    bit = part // 4
+    f32 = jnp.float32
+
+    def kernel(out_ref, gtok_ref, eq_ref, eo_ref, eu_ref, ed_ref, fs_ref, fb_ref, *ends):
+        ends[0][...] = out_ref[...]
+        ends[1][...] = gtok_ref[...]
+        deep, wide = eq_ref.shape[1], eu_ref.shape[2]
+        for member in range(4):
+            ends[2][:, member * deep : (member + 1) * deep] = eq_ref[member].astype(f32).T
+            ends[4][:, member * wide : (member + 1) * wide] = eu_ref[member].astype(f32)
+        ends[3][...] = eo_ref[...].reshape(ends[3].shape).astype(f32)
+        ends[5][...] = ed_ref[...].reshape(ends[5].shape).astype(f32)
+        z = lax.axis_index("tensor")
+        mine = fs_ref[:, 0:bit]
+        for plane in range(1, 4):
+            mine = jnp.where(z == plane, fs_ref[:, plane * bit : (plane + 1) * bit], mine)
+        for row in range(6):
+            ends[6 + row][...] = mine[row]
+        dp, deep = lax.axis_index("dp"), part // 16
+        for end, first, count in ((ends[12], 0, 1), (ends[13], 1, 2)):
+            spread = jnp.concatenate(
+                [
+                    jnp.broadcast_to(fb_ref[member, first + half : first + half + 1, :], (deep, part))
+                    for member in range(4)
+                    for half in range(count)
+                ]
+            )
+            row = lax.broadcasted_iota(jnp.int32, spread.shape, 0) % deep
+            lane = lax.broadcasted_iota(jnp.int32, spread.shape, 1)
+            for side in range(2):
+                kept = jnp.where(lane == row * 16 + 2 * dp + side, spread, 0.0)
+                end[side : side + 1, :] = lax.dot_general(
+                    jnp.ones((1, part), f32),
+                    kept,
+                    (((1,), (1,)), ((), ())),
+                    precision=lax.Precision.HIGHEST,
+                    preferred_element_type=f32,
+                )
+
+    shapes = [
+        out,
+        gtok,
+        jax.ShapeDtypeStruct((part, 4 * eq.shape[1]), f32),
+        jax.ShapeDtypeStruct((4 * eo.shape[1], part), f32),
+        jax.ShapeDtypeStruct((part, 4 * eu.shape[2]), f32),
+        jax.ShapeDtypeStruct((4 * ed.shape[1], part), f32),
+    ] + [jax.ShapeDtypeStruct((bit,), f32)] * 6
+    shapes += [jax.ShapeDtypeStruct((2, size), f32) for size in (part // 4, part // 2)]
+    return pl.pallas_call(
+        kernel,
+        out_shape=[jax.ShapeDtypeStruct(shape.shape, shape.dtype) for shape in shapes],
+        in_specs=[pl.BlockSpec(memory_space=pltpu.VMEM)] * 8,
+        out_specs=[pl.BlockSpec(memory_space=pltpu.VMEM)] * 14,
+        name="finish",
+    )(out, gtok, eq, eo, eu, ed, fs, fb)
+
+
 SEMS = 256
 VMEM_LIMIT = 67043328
 
@@ -1478,18 +1542,10 @@
     out, gtok, eq, eo, eu, ed, fs, fb = fused_layer(
         tokens_in, grad_out, in_q, in_o, w_up, in_d, si
     )
-    grad_w_qkv = eq.transpose(2, 0, 1).reshape(part, 3 * 4 * dim).astype(f32)
-    grad_w_out = eo.reshape(4 * dim, part).astype(f32)
-    grad_w_up = eu.transpose(1, 0, 2).reshape(part, 4 * hidden).astype(f32)
-    grad_w_down = ed.reshape(4 * hidden, part).astype(f32)
-    take = lax.dynamic_slice_in_dim(fs, z * bit, bit, 1)
-
-    def collect(rows, like):
-        entries = rows.reshape(4, -1, 8, like.shape[1])
-        return lax.dynamic_index_in_dim(entries, dp, 2, keepdims=False).reshape(like.shape)
-
-    grad_b_qv = collect(fb[:, 0], b_qv)
-    grad_b_up = collect(fb[:, 1:3], b_up)
+    out, gtok, grad_w_qkv, grad_w_out, grad_w_up, grad_w_down, *take = finish(
+        out, gtok, eq, eo, eu, ed, fs, fb
+    )
+    grad_b_qv, grad_b_up = take[6].T, take[7].T
     return (
         out, gtok, take[0], take[1], grad_w_qkv, grad_b_qv, grad_w_out, take[2],
         take[3], take[4], grad_w_up, grad_b_up, grad_w_down, take[5],

time: 239 us -> 229 us (0.958)
  local copies, waits for them, and re-layouts: 12.8 us -> 4.49 us
    unnamed x39 -> x21, local copies, waits for them, and re-layouts: 7.65 us -> 3.29 us
    pallas_call x0 -> x1, Pallas kernels: none -> 3.27 us  [finish(): pl.pallas_call(kernel, out_shape=[jax.ShapeDtypeStruct(shape.shape, shape...]
    pallas_call x1, Pallas kernels: 222 us -> 219 us  [fused_layer(): pl.pallas_call(kernel, out_shape=(jax.ShapeDtypeStruct((rows, width), low...]
where the time goes in v5:
time: 229 us
  Pallas kernels  222 us (97%)
  local copies, waits for them, and re-layouts  4.49 us (2%)
    pallas_call x1, Pallas kernels, fused_layer(): pl.pallas_call(kernel, out_shape=(jax.ShapeDtypeStruct((rows, width), low...  219 us

profile of v5, /device:TPU:1, one launch (start us, length us, event | category | flops | bytes accessed | tf_op | source)
XLA Modules:
  0.0 228.5 jit_solution(2023355433006560446)
XLA Ops:
  0.7 0.0 copy-start.9
  0.7 0.6 copy-done.9
  1.3 0.0 copy-start.1
  1.3 0.0 copy-start.2
  1.4 0.0 copy-start.3
  1.4 0.0 copy-start.4
  1.4 0.0 copy-start.5
  1.4 0.0 copy-start.6
  1.4 0.1 pad.8.clone
  1.5 0.5 copy-done.1
  2.0 0.0 copy-done.2
  2.0 0.0 copy-done.3
  2.0 0.0 copy-done.4
  2.0 0.0 copy-done.5
  2.1 0.0 copy-done.6
  2.1 0.0 copy-start.7
  2.1 0.6 copy-done.7
  2.7 0.1 reshape.86
  2.8 0.0 copy-start.8
  2.8 0.1 copy.33
  2.9 0.6 copy-done.8
  3.5 0.1 reshape.87
  3.6 0.1 tile.10
  3.7 0.1 broadcast_in_dim.85
  3.7 0.1 broadcast_in_dim.86
  3.9 0.1 copy.35
  4.0 0.1 broadcast_in_dim.93
  4.1 0.2 broadcast_in_dim.94
  4.2 0.0 copy-start
  4.3 0.1 copy.34
  4.3 0.1 broadcast_in_dim.98
  4.4 0.1 copy.36
  4.5 0.7 maximum_maximum_fusion.refs_6_
  5.2 0.0 copy-done
  5.2 0.8 copy.32
  6.0 219.1 %fused_layer.1 = (bf16[256,1024]{1,0:T(8,128)(2,1)}, bf16[256,1024]{1,0:T(8,128)(2,1)}, bf16[4,192,128]{2,1,0:T(8,128)(2,1)}, bf16[4,64,128]{2,1,0:T(8,128)(2,1)...) custom-call(bf16[256,1024]{1,0:T(8,128)(2,1)} %refs_0_.1, ...), custom_call_target="tpu_custom_call" | custom-call | tf_op jit(solution)/shard_map/fused_layer/pallas_call | solution.py:1425
  225.1 3.3 %finish.1 = (bf16[256,1024]{1,0:T(8,128)(2,1)}, bf16[256,1024]{1,0:T(8,128)(2,1)}, f32[128,768]{1,0:T(8,128)}, f32[256,128]{1,0:T(8,128)}, f32[128,1024]{1,0:T(8...) custom-call(bf16[256,1024]{1,0:T(8,128)(2,1)} %get-tuple-element.36., ...), custom_call_target="tpu_custom_call" | custom-call | tf_op jit(solution)/shard_map/finish/pallas_call | solution.py:1500
  (11 shorter events, 0.1 us)
Async XLA Ops:
  0.7 0.7 copy-start.9
  1.3 0.7 copy-start.1
  1.3 0.7 copy-start.2
  1.4 0.7 copy-start.3
  1.4 0.7 copy-start.4
  1.4 0.7 copy-start.5
  1.4 0.7 copy-start.6
  2.1 0.7 copy-start.7
  2.8 0.7 copy-start.8
  4.2 0.9 copy-start

commit v6 on v5

--- a/solution.py
+++ b/solution.py
@@ -344,7 +344,7 @@
 MESH = pl.DeviceIdType.MESH
 CH = 2
 HOPS = 4
-RELAYED = "ud"
+RELAYED = "qud"
 
 
 class Fused:

time: 229 us -> 226 us (0.987)
  Pallas kernels: 222 us -> 219 us
    pallas_call x1, Pallas kernels: 219 us -> 215 us  [fused_layer(): pl.pallas_call(kernel, out_shape=(jax.ShapeDtypeStruct((rows, width), low...]
where the time goes in v6:
time: 226 us; the launch traced here: 225 us
  Pallas kernels  219 us (97%)
  local copies, waits for them, and re-layouts  4.49 us (2%)
    pallas_call x1, Pallas kernels, fused_layer(): pl.pallas_call(kernel, out_shape=(jax.ShapeDtypeStruct((rows, width), low...  215 us

profile of v6, /device:TPU:1, one launch (start us, length us, event | category | flops | bytes accessed | tf_op | source)
XLA Modules:
  0.0 224.7 jit_solution(4890010608567348569)
XLA Ops:
  0.7 0.0 copy-start.9
  0.7 0.6 copy-done.9
  1.3 0.0 copy-start.1
  1.3 0.0 copy-start.2
  1.4 0.0 copy-start.3
  1.4 0.0 copy-start.4
  1.4 0.0 copy-start.5
  1.4 0.0 copy-start.6
  1.4 0.1 pad.8.clone
  1.5 0.5 copy-done.1
  2.0 0.0 copy-done.2
  2.0 0.0 copy-done.3
  2.0 0.0 copy-done.4
  2.0 0.0 copy-done.5
  2.1 0.0 copy-done.6
  2.1 0.0 copy-start.7
  2.1 0.6 copy-done.7
  2.7 0.1 reshape.86
  2.8 0.0 copy-start.8
  2.8 0.1 copy.33
  2.9 0.6 copy-done.8
  3.5 0.1 reshape.87
  3.6 0.1 tile.10
  3.7 0.1 broadcast_in_dim.85
  3.7 0.1 broadcast_in_dim.86
  3.9 0.1 copy.35
  4.0 0.1 broadcast_in_dim.93
  4.1 0.2 broadcast_in_dim.94
  4.2 0.0 copy-start
  4.3 0.1 copy.34
  4.3 0.1 broadcast_in_dim.98
  4.4 0.1 copy.36
  4.5 0.7 maximum_maximum_fusion.refs_6_
  5.2 0.0 copy-done
  5.2 0.8 copy.32
  6.0 215.3 %fused_layer.1 = (bf16[256,1024]{1,0:T(8,128)(2,1)}, bf16[256,1024]{1,0:T(8,128)(2,1)}, bf16[4,192,128]{2,1,0:T(8,128)(2,1)}, bf16[4,64,128]{2,1,0:T(8,128)(2,1)...) custom-call(bf16[256,1024]{1,0:T(8,128)(2,1)} %refs_0_.1, ...), custom_call_target="tpu_custom_call" | custom-call | tf_op jit(solution)/shard_map/fused_layer/pallas_call | solution.py:1425
  221.3 3.3 %finish.1 = (bf16[256,1024]{1,0:T(8,128)(2,1)}, bf16[256,1024]{1,0:T(8,128)(2,1)}, f32[128,768]{1,0:T(8,128)}, f32[256,128]{1,0:T(8,128)}, f32[128,1024]{1,0:T(8...) custom-call(bf16[256,1024]{1,0:T(8,128)(2,1)} %get-tuple-element.36., ...), custom_call_target="tpu_custom_call" | custom-call | tf_op jit(solution)/shard_map/finish/pallas_call | solution.py:1500
  (11 shorter events, 0.1 us)
Async XLA Ops:
  0.7 0.7 copy-start.9
  1.3 0.7 copy-start.1
  1.3 0.7 copy-start.2
  1.4 0.7 copy-start.3
  1.4 0.7 copy-start.4
  1.4 0.7 copy-start.5
  1.4 0.7 copy-start.6
  2.1 0.7 copy-start.7
  2.8 0.7 copy-start.8
  4.2 0.9 copy-start
